TPU v7x, 8 devices: a whole 2x2x1 slice. The times are simulated.
8 devices in a mesh: replica: 2 (over z, y), data: 4 (over x, core).
Axes of the slice: x: 2, y: 2, z: 1, core: 2. Of those that a mesh axis runs over, the one named last changes fastest.
Arguments:
- x_seq: bfloat16 [256, 16, 2048], P(('replica', 'data'))
- dy_seq: float32 [256, 16, 2048], P(('replica', 'data'))
- w_stack: bfloat16 [2, 4096, 8192], replicated
- b_stack: float32 [2, 8192], replicated
Outputs:
- output 1: float32 [2, 4096, 8192], replicated
- output 2: float32 [2, 8192], replicated
- output 3: float32 [256, 16, 2048], P(('replica', 'data'))
All inputs are finite; a program needn't handle non-finite values.
Results may differ from a plain program's by a relative error of at most 0.0129304.
Values are sent between devices in bfloat16 or wider.
A program may use at most 1.75 GiB of HBM per device.

v0:
```python
import jax
import jax.numpy as jnp
from jax import lax
from jax.sharding import PartitionSpec as P


def layer_forward(u_seq, w_layer, b_layer):
    hidden = u_seq.shape[-1]
    batch_rows = u_seq.shape[1]
    w_rec = w_layer[hidden:]
    in_proj = jnp.einsum('tbh,hg->tbg', u_seq, w_layer[:hidden], preferred_element_type=jnp.float32) + b_layer

    def time_step(carry_state, z_in):
        h_prev, c_prev = carry_state
        z_all = z_in + jnp.dot(h_prev, w_rec, preferred_element_type=jnp.float32)
        z_i, z_f, z_g, z_o = jnp.split(z_all, 4, axis=-1)
        gate_i = jax.nn.sigmoid(z_i)
        gate_f = jax.nn.sigmoid(z_f)
        gate_g = jnp.tanh(z_g)
        gate_o = jax.nn.sigmoid(z_o)
        c_new = gate_f * c_prev + gate_i * gate_g
        tanh_c = jnp.tanh(c_new)
        h_new = (gate_o * tanh_c).astype(jnp.bfloat16)
        return (h_new, c_new), (h_new, c_new, tanh_c, gate_i, gate_f, gate_g, gate_o)

    init_state = (jnp.zeros((batch_rows, hidden), jnp.bfloat16), jnp.zeros((batch_rows, hidden), jnp.float32))
    return lax.scan(time_step, init_state, in_proj)[1]


def layer_backward(u_seq, w_layer, saved_acts, dh_seq):
    hidden = u_seq.shape[-1]
    h_seq, c_seq, tanh_seq, i_seq, f_seq, g_seq, o_seq = saved_acts
    h_prev_seq = jnp.concatenate([jnp.zeros_like(h_seq[:1]), h_seq[:-1]], axis=0)
    c_prev_seq = jnp.concatenate([jnp.zeros_like(c_seq[:1]), c_seq[:-1]], axis=0)
    w_rec = w_layer[hidden:]

    def time_step(carry_state, step_in):
        dh_rec, dc_next = carry_state
        dh_out, c_prev, tanh_c, gate_i, gate_f, gate_g, gate_o = step_in
        dh_tot = dh_out + dh_rec
        dc_cur = dc_next + dh_tot * gate_o * (1.0 - tanh_c * tanh_c)
        dz_all = jnp.concatenate([dc_cur * gate_g * gate_i * (1.0 - gate_i), dc_cur * c_prev * gate_f * (1.0 - gate_f), dc_cur * gate_i * (1.0 - gate_g * gate_g), dh_tot * tanh_c * gate_o * (1.0 - gate_o)], axis=-1)
        dz_low = dz_all.astype(jnp.bfloat16)
        dh_prev = jnp.einsum('bg,hg->bh', dz_low, w_rec, preferred_element_type=jnp.float32)
        return (dh_prev, dc_cur * gate_f), (dz_low, jnp.sum(dz_all, axis=0))

    init_state = (jnp.zeros_like(dh_seq[0]), jnp.zeros_like(dh_seq[0]))
    dz_seq, db_steps = lax.scan(time_step, init_state, (dh_seq, c_prev_seq, tanh_seq, i_seq, f_seq, g_seq, o_seq), reverse=True)[1]
    dx_seq = jnp.einsum('tbg,hg->tbh', dz_seq, w_layer[:hidden], preferred_element_type=jnp.float32)
    dw_in = jnp.einsum('tbh,tbg->hg', u_seq, dz_seq, preferred_element_type=jnp.float32)
    dw_rec = jnp.einsum('tbh,tbg->hg', h_prev_seq, dz_seq, preferred_element_type=jnp.float32)
    return jnp.concatenate([dw_in, dw_rec], axis=0), jnp.sum(db_steps, axis=0), dx_seq


def reduce_weights(dw_part):
    part_low = dw_part.astype(jnp.bfloat16)
    shard_sum = lax.psum_scatter(part_low, 'data', scatter_dimension=0, tiled=True)
    shard_sum = lax.psum(shard_sum, 'replica')
    return lax.all_gather(shard_sum, 'data', axis=0, tiled=True).astype(jnp.float32)


def solution(mesh):
    batch_axes = ('replica', 'data')

    def local_grads(x_loc, dy_loc, w_stack, b_stack):
        layers = w_stack.shape[0]
        u_seq = jnp.swapaxes(x_loc, 0, 1)
        layer_inputs = []
        layer_saved = []
        for layer_idx in range(layers):
            saved_acts = layer_forward(u_seq, w_stack[layer_idx], b_stack[layer_idx])
            layer_inputs.append(u_seq)
            layer_saved.append(saved_acts)
            u_seq = saved_acts[0]
        dh_seq = jnp.swapaxes(dy_loc, 0, 1)
        dw_list = []
        db_list = []
        for layer_idx in reversed(range(layers)):
            dw_part, db_part, dh_seq = layer_backward(layer_inputs[layer_idx], w_stack[layer_idx], layer_saved[layer_idx], dh_seq)
            dw_list.append(reduce_weights(dw_part))
            db_list.append(lax.psum(db_part.astype(jnp.bfloat16), batch_axes).astype(jnp.float32))
        return jnp.stack(dw_list[::-1]), jnp.stack(db_list[::-1]), jnp.swapaxes(dh_seq, 0, 1)

    return jax.shard_map(local_grads, mesh=mesh, in_specs=(P(batch_axes), P(batch_axes), P(), P()), out_specs=(P(), P(), P(batch_axes)), check_vma=False)
```

profile of v0, /device:TPU:0, one launch (start us, length us, event | category | flops | bytes accessed | tf_op | source)
XLA Modules:
  0.0 3640.3 jit_solution(16549847835187771421)
XLA Ops:
  14.9 43.8 %slice_bitcast_fusion = (bf16[2048,8192]{1,0:T(8,128)(2,1)}, bf16[2048,8192]{1,0:T(8,128)(2,1)}) fusion(bf16[2,4096,8192]{2,1,0:T(8,128)(2,1)} %param.14), kind=kLoop, calls=%fused_computation.137 | loop fusion | bytes 134217728 | tf_op jit(solution)/shard_map/slice | solution.py:10
  58.6 28.6 fusion.69
  102.4 256.0 %while.96 = (s32[]{:T(128)}, bf16[32,2048]{1,0:T(8,128)(2,1)S(1)}, f32[32,2048]{1,0:T(8,128)S(1)}, bf16[16,32,2048]{2,1,0:T(8,128)(2,1)S(1)}, f32[16,32,2048]{2,...) while((s32[]{:T(128)}, bf16[32,2048]{1,0:T(8,128)(2,1)S(1)}, ...), condition=%wide.region_1.2_spmd.clone, body=%wide.region_0.1_spmd.clone.sunk | while | flops 1075249152 | bytes 39977124 | solution.py:27
  358.5 25.7 fusion.72
  400.7 265.8 %while.97 = (s32[]{:T(128)}, bf16[32,2048]{1,0:T(8,128)(2,1)S(1)}, f32[32,2048]{1,0:T(8,128)S(1)}, bf16[16,32,2048]{2,1,0:T(8,128)(2,1)}, f32[16,32,2048]{2,1,0:...) while((s32[]{:T(128)}, bf16[32,2048]{1,0:T(8,128)(2,1)S(1)}, ...), condition=%wide.region_3.4_spmd.clone, body=%wide.region_2.3_spmd.clone.sunk | while | flops 1075249152 | bytes 39977124 | solution.py:27
  676.6 329.9 %while.98 = (s32[]{:T(128)}, f32[32,2048]{1,0:T(8,128)S(1)}, f32[32,2048]{1,0:T(8,128)S(1)}, bf16[16,32,8192]{2,1,0:T(8,128)(2,1)}, f32[16,8192]{1,0:T(8,128)}, ...) while((s32[]{:T(128)}, f32[32,2048]{1,0:T(8,128)S(1)}, ...), condition=%wide.region_6.7_spmd.clone, body=%wide.region_4.6_spmd.clone.sunk | while | flops 1080811520 | bytes 42303680 | solution.py:48
  679.8 15.1 fusion.125
  700.4 15.1 fusion.125
  721.0 15.1 fusion.125
  741.6 15.1 fusion.125
  762.2 15.1 fusion.125
  803.3 15.1 fusion.125
  824.0 15.1 fusion.125
  844.5 15.1 fusion.125
  865.1 15.1 fusion.125
  885.7 15.1 fusion.125
  906.3 15.1 fusion.125
  926.9 15.1 fusion.125
  947.5 15.1 fusion.125
  968.1 15.1 fusion.125
  988.8 15.1 fusion.125
  1006.5 25.2 bitcast_convert_fusion.1
  1031.7 23.3 bitcast_convert_fusion
  1055.0 45.4 %pad_maximum_fusion.3 = bf16[4096,8192]{1,0:T(8,128)(2,1)} fusion(bf16[2048,8192]{1,0:T(8,128)(2,1)} %bitcast_convert_fusion, bf16[2048,8192]{1,0:T(8,128)(2,1)} %bitcast_convert_fusion.1), kind=kLoop, calls=%fused_computation.124 | loop fusion | flops 134217728 | bytes 134217728 | tf_op jit(solution)/shard_map/concatenate | solution.py:52
  1106.9 22.6 fusion.56
  1133.8 303.9 %while.99 = (s32[]{:T(128)}, f32[32,2048]{1,0:T(8,128)S(1)}, f32[32,2048]{1,0:T(8,128)S(1)}, bf16[16,32,8192]{2,1,0:T(8,128)(2,1)}, f32[16,8192]{1,0:T(8,128)S(1...) while((s32[]{:T(128)}, f32[32,2048]{1,0:T(8,128)S(1)}, ...), condition=%wide.region_9.10_spmd.clone, body=%wide.region_7.9_spmd.clone.sunk | while | flops 1080811520 | bytes 42303680 | solution.py:48
  1136.6 15.1 fusion.129
  1174.6 15.1 fusion.129
  1212.6 15.1 fusion.129
  1231.6 15.1 fusion.129
  1250.6 15.1 fusion.129
  1288.6 15.1 fusion.129
  1326.6 15.1 fusion.129
  1345.6 15.1 fusion.129
  1364.6 15.1 fusion.129
  1383.6 15.1 fusion.129
  1402.6 15.1 fusion.129
  1421.6 15.1 fusion.129
  1437.7 26.0 fusion.68
  1463.7 23.5 bitcast_convert_fusion.2
  1487.2 45.4 %pad_maximum_fusion.2 = bf16[4096,8192]{1,0:T(8,128)(2,1)} fusion(bf16[2048,8192]{1,0:T(8,128)(2,1)} %bitcast_convert_fusion.2, bf16[2048,8192]{1,0:T(8,128)(2,1)} %fusion.68), kind=kLoop, calls=%fused_computation.123 | loop fusion | flops 134217728 | bytes 134217728 | tf_op jit(solution)/shard_map/concatenate | solution.py:52
  1543.9 443.1 %reduce-scatter.7.cloned.1.call-done = bf16[1024,8192]{1,0:T(8,128)(2,1)} async-done(((bf16[4096,8192]{1,0:T(8,128)(2,1)}), bf16[1024,8192]{1,0:T(8,128)(2,1)}) %reduce-scatter.7.cloned.1.call-update) | async-done | bytes 16777232
  1987.1 734.3 %all-reduce.10.cloned.1.call-done = (bf16[1024,8192]{1,0:T(8,128)(2,1)}, bf16[1024,8192]{1,0:T(8,128)(2,1)}) async-done(((bf16[1024,8192]{1,0:T(8,128)(2,1)}, bf16[1024,8192]{1,0:T(8,128)(2,1)}), (bf16[1024,8192]{1,0:T(8,128)(2,1)}, bf16[1024,8192]{1,0:T(8,128)(2,1)})) %all-reduce.10.cloned.1.call-update) | async-done | bytes 33554448 | tf_op jit(solution)/shard_map/psum | solution.py:58
  2722.7 23.9 fusion.75
  2751.1 24.8 all-reduce.6
  2776.5 338.7 %all-gather.5.cloned.1.call-done = bf16[4096,8192]{1,0:T(8,128)(2,1)} async-done(((bf16[1024,8192]{1,0:T(8,128)(2,1)}), bf16[4096,8192]{1,0:T(8,128)(2,1)}) %all-gather.5.cloned.1.call-update) | async-done | bytes 67108880 | tf_op jit(solution)/shard_map/all_gather | solution.py:59
  3115.3 391.1 %all-gather.3.cloned.1.call-done = bf16[4096,8192]{1,0:T(8,128)(2,1)} async-done(((bf16[1024,8192]{1,0:T(8,128)(2,1)}), bf16[4096,8192]{1,0:T(8,128)(2,1)}) %all-gather.3.cloned.1.call-update) | async-done | bytes 67108880 | tf_op jit(solution)/shard_map/all_gather | solution.py:59
  3506.4 127.2 %maximum_convert_fusion = f32[2,4096,8192]{2,1,0:T(8,128)} fusion(bf16[1,4096,8192]{2,1,0:T(8,128)(2,1)} %bitcast.16, bf16[1,4096,8192]{2,1,0:T(8,128)(2,1)} %bitcast.13), kind=kLoop, calls=%fused_computation.122 | loop fusion | flops 134217728 | bytes 402653184 | tf_op jit(solution)/shard_map/stack | solution.py:82
  (363 shorter events, 823.3 us)
Async XLA Ops:
  7.2 1536.7 %reduce-scatter.9.cloned.1.call-start = ((), (), s32[]{:S(2)}) async-start(), calls=%async_computation.5 | async-start | bytes 83886080
  14.9 43.8 %copy-start.7 = (bf16[32,16,2048]{2,1,0:T(8,128)(2,1)S(1)}, bf16[32,16,2048]{2,1,0:T(8,128)(2,1)}, u32[]{:S(2)}) copy-start(bf16[32,16,2048]{2,1,0:T(8,128)(2,1)} %param.12) | copy-start | bytes 6291460
  358.5 648.1 %copy-start.5 = (bf16[16,32,2048]{2,1,0:T(8,128)(2,1)}, bf16[16,32,2048]{2,1,0:T(8,128)(2,1)S(1)}, u32[]{:S(2)}) copy-start(bf16[16,32,2048]{2,1,0:T(8,128)(2,1)S(1)} %get-tuple-element.651) | copy-start | bytes 6291460
  395.6 5.1 copy-start
  395.6 5.1 copy-start.4
  672.3 4.3 copy-start.3
  1006.5 25.2 copy-start.2
  1100.4 886.7 %reduce-scatter.7.cloned.1.call-start = ((), (), s32[]{:S(2)}) async-start(), calls=%async_computation.4 | async-start | bytes 83886080
  1100.4 5.2 slice-start
  1103.0 3.9 slice-start.1
  1437.7 26.0 copy-start.1
  1532.6 1188.8 %all-reduce.10.cloned.1.call-start = ((), (), s32[]{:S(2)}) async-start(), calls=%async_computation.6 | async-start | bytes 67108864 | tf_op jit(solution)/shard_map/psum | solution.py:58
  1987.0 1128.2 %all-gather.5.cloned.1.call-start = ((), (), s32[]{:S(2)}) async-start(), calls=%async_computation.3 | async-start | bytes 83886080 | tf_op jit(solution)/shard_map/all_gather | solution.py:59
  2721.4 785.0 %all-gather.3.cloned.1.call-start = ((), (), s32[]{:S(2)}) async-start(), calls=%async_computation.2 | async-start | bytes 83886080 | tf_op jit(solution)/shard_map/all_gather | solution.py:59
  2721.4 1.0 copy-start.6
Sparse Core Ops, SparseCore 0:
  1100.5 443.3 reduce-scatter.8
  1546.4 440.5 reduce-scatter.6
  1989.5 731.8 all-reduce.9
  2722.8 392.4 all-gather.4
  3116.7 389.6 all-gather.2
where the time goes:
time: 3650 us; the launch traced here: 3640 us
  waiting for transfers between devices  1920 us (53%)
  matrix products  1130 us (31%)
  other arithmetic  388 us (11%)
  local copies, waits for them, and re-layouts  163 us (4%)
    psum x1, waiting for transfers between devices, reduce_weights(): shard_sum = lax.psum(shard_sum, 'replica')  734 us
    all_gather x2, waiting for transfers between devices, reduce_weights(): lax.all_gather(shard_sum, 'data', axis=0, tiled=True).astype(jnp.float32)  730 us
    dot_general x32, matrix products, time_step(): jnp.einsum('bg,hg->bh', dz_low, w_rec, preferred_element_type=jnp.float32)  484 us
    unnamed x7, waiting for transfers between devices  455 us
    dot_general x32, matrix products, time_step(): z_all = z_in + jnp.dot(h_prev, w_rec, preferred_element_type=jnp.float32)  446 us
    another operation x1, other arithmetic, local_grads(): jnp.stack(dw_list[::-1])  127 us
    concatenate x2, other arithmetic, layer_backward(): jnp.concatenate([dw_in, dw_rec], axis=0)  90.8 us
    concatenate x64, other arithmetic, time_step(): jnp.concatenate([dc_cur * gate_g * gate_i * (1.0 - gate_i), dc_cur * c_pr...  86.9 us
  transfers between devices with their start and end apart: 5, of which 5 were waited for; matrix products, arithmetic and copies ran while one was open for 13% of the time, Pallas kernels for 0%

commit v1 on v0

v1 whole, which is shorter than its diff:
```python
import functools

import jax
import jax.numpy as jnp
from jax import lax
from jax.experimental import pallas as pl
from jax.experimental.pallas import tpu as pltpu
from jax.sharding import PartitionSpec as P


VMEM_BYTES = 67043328
BF16, F32 = jnp.bfloat16, jnp.float32


def dot(a, b):
    return jnp.dot(a, b, preferred_element_type=F32)


def forward_kernel(layer, rows, steps, in_blk, n_blk, u_hbm, win_ref, b_ref, w_hbm, acts_ref, h_hbm, ht_hbm, wt_hbm, wrec, zin, uh, c_scr, wt_buf, ht_buf, sem_w, sem_u, sem_o):
    hidden = uh.shape[1]
    n_in = 4 * hidden // in_blk
    cut = hidden // steps
    i = pl.program_id(0)
    part = hidden // 8

    def w_copy(k):
        return pltpu.make_async_copy(w_hbm.at[layer, pl.ds(hidden + k * part, part)], wrec.at[pl.ds(k * part, part)], sem_w.at[k])

    def wt_copy(t):
        return pltpu.make_async_copy(wt_buf, wt_hbm.at[:, pl.ds(pl.multiple_of(t * cut, cut), cut)], sem_o.at[0])

    @pl.when(i == 0)
    def _():
        u_copy = pltpu.make_async_copy(u_hbm, uh, sem_u)
        u_copy.start()
        for k in range(8):
            w_copy(k).start()
        u_copy.wait()

    @pl.when(i < n_in)
    def _():
        zin[:, pl.ds(pl.multiple_of(i * in_blk, in_blk), in_blk)] = dot(uh[...], win_ref[0]) + b_ref[...]

    def step(t, first):
        now = pl.ds(pl.multiple_of(t * rows, rows), rows)
        wt_buf[...] = wrec[pl.ds(pl.multiple_of(t * cut, cut), cut), :].T
        h_prev = None if first else uh[pl.ds(pl.multiple_of((t - 1) * rows, rows), rows), :]
        for n0 in range(0, hidden, n_blk):
            cols = pl.ds(n0, n_blk)
            z = []
            for g in range(4):
                gcols = pl.ds(g * hidden + n0, n_blk)
                zg = zin[now, gcols]
                z.append(zg if first else zg + dot(h_prev, wrec[:, gcols]))
            gate_i, gate_f, gate_g, gate_o = jax.nn.sigmoid(z[0]), jax.nn.sigmoid(z[1]), jnp.tanh(z[2]), jax.nn.sigmoid(z[3])
            c_new = gate_i * gate_g if first else gate_f * c_scr[:, cols] + gate_i * gate_g
            tanh_c = jnp.tanh(c_new)
            c_scr[:, cols] = c_new
            uh[now, cols] = (gate_o * tanh_c).astype(BF16)
            for k, a in enumerate((gate_i, gate_f, gate_g, gate_o, tanh_c, c_new)):
                acts_ref[k, :, cols] = a

    @pl.when(i == n_in)
    def _():
        for k in range(8):
            w_copy(k).wait()
        step(0, True)
        wt_copy(0).start()

    @pl.when(i > n_in)
    def _():
        t = i - n_in
        wt_copy(t - 1).wait()
        step(t, False)
        wt_copy(t).start()

    @pl.when(i == n_in + steps - 1)
    def _():
        h_copy = pltpu.make_async_copy(uh, h_hbm, sem_u)
        h_copy.start()
        for k in range(8):
            ht_buf[pl.ds(k * part, part), :] = uh[:, pl.ds(k * part, part)].T
        ht_copy = pltpu.make_async_copy(ht_buf, ht_hbm, sem_o.at[1])
        ht_copy.start()
        wt_copy(steps - 1).wait()
        h_copy.wait()
        ht_copy.wait()


def forward(layer, u, w_stack, b_stack, rows, steps):
    total, hidden = u.shape
    in_blk, n_blk = hidden // 4, hidden // 4
    n_in = 4 * hidden // in_blk
    t_of = lambda i: jnp.maximum(i - n_in, 0)
    k_of = lambda i: jnp.minimum(i, n_in - 1)
    return pl.pallas_call(
        functools.partial(forward_kernel, layer, rows, steps, in_blk, n_blk),
        grid=(n_in + steps,),
        in_specs=[
            pl.BlockSpec(memory_space=pl.ANY),
            pl.BlockSpec((1, hidden, in_blk), lambda i: (layer, 0, k_of(i))),
            pl.BlockSpec((1, in_blk), lambda i: (0, k_of(i))),
            pl.BlockSpec(memory_space=pl.ANY),
        ],
        out_specs=[
            pl.BlockSpec((6, rows, hidden), lambda i: (0, t_of(i), 0)),
            pl.BlockSpec(memory_space=pl.ANY),
            pl.BlockSpec(memory_space=pl.ANY),
            pl.BlockSpec(memory_space=pl.ANY),
        ],
        out_shape=[
            jax.ShapeDtypeStruct((6, total, hidden), F32),
            jax.ShapeDtypeStruct((total, hidden), BF16),
            jax.ShapeDtypeStruct((hidden, total), BF16),
            jax.ShapeDtypeStruct((4 * hidden, hidden), BF16),
        ],
        scratch_shapes=[
            pltpu.VMEM((hidden, 4 * hidden), BF16),
            pltpu.VMEM((total, 4 * hidden), F32),
            pltpu.VMEM((total, hidden), BF16),
            pltpu.VMEM((rows, hidden), F32),
            pltpu.VMEM((4 * hidden, hidden // steps), BF16),
            pltpu.VMEM((hidden, total), BF16),
            pltpu.SemaphoreType.DMA((8,)),
            pltpu.SemaphoreType.DMA,
            pltpu.SemaphoreType.DMA((2,)),
        ],
        compiler_params=pltpu.CompilerParams(dimension_semantics=("arbitrary",), vmem_limit_bytes=VMEM_BYTES),
        cost_estimate=pl.CostEstimate(flops=4 * total * hidden * 4 * hidden, bytes_accessed=4 * hidden * hidden * 4 * 3, transcendentals=0),
    )(u, w_stack, b_stack[layer][None], w_stack)


def backward_kernel(carried, rows, t_top, n_e, widths, n_blk, *refs):
    refs = list(refs)
    e_refs = [refs.pop(0) for _ in range(n_e)]
    acts_ref, cprev_ref = refs.pop(0), refs.pop(0)
    if carried:
        dz_in, fdc_in, db_in = refs.pop(0), refs.pop(0), refs.pop(0)
    wt_hbm = refs.pop(0)
    dz_ref = refs.pop(0)
    starts = [sum(widths[:k]) for k in range(len(widths))]
    chunk_refs = [refs.pop(0) for _ in widths]
    fdc_ref, db_ref, wt, dz_scr, sem_w = refs
    hidden = fdc_ref.shape[1]
    part = hidden // 8
    s = pl.program_id(0)
    t = t_top - s

    def w_copy(k):
        return pltpu.make_async_copy(wt_hbm.at[pl.ds(k * 4 * part, 4 * part)], wt.at[pl.ds(k * 4 * part, 4 * part)], sem_w.at[k])

    def step(first):
        new, old = lax.rem(s, 2), lax.rem(s + 1, 2)
        later = None if first else dz_scr[old]
        for n0 in range(0, hidden, n_blk):
            cols = pl.ds(n0, n_blk)
            gate_i, gate_f, gate_g, gate_o, tanh_c = (acts_ref[k, :, cols] for k in range(5))
            c_prev = jnp.where(t > 0, cprev_ref[0, :, cols], 0.0)
            dh = e_refs[0][:, cols]
            if n_e > 1:
                dh = jnp.where(t < 8, dh, e_refs[1][:, cols])
            if not first:
                dh = dh + dot(later, wt[:, cols])
            dc = dh * gate_o * (1.0 - tanh_c * tanh_c)
            if not first:
                dc = fdc_ref[:, cols] + dc
            fdc_ref[:, cols] = dc * gate_f
            dz = (
                dc * gate_g * gate_i * (1.0 - gate_i),
                dc * c_prev * gate_f * (1.0 - gate_f),
                dc * gate_i * (1.0 - gate_g * gate_g),
                dh * tanh_c * gate_o * (1.0 - gate_o),
            )
            for k in range(4):
                at = k * hidden + n0
                gcols = pl.ds(at, n_blk)
                low = dz[k].astype(BF16)
                dz_scr[new, :, gcols] = low
                dz_ref[:, gcols] = low
                for ref, start in zip(chunk_refs, starts):
                    if start <= at < start + ref.shape[1]:
                        ref[:, pl.ds(at - start, n_blk)] = low
                part_sum = dz[k][0:8]
                for q in range(8, rows, 8):
                    part_sum = part_sum + dz[k][q : q + 8]
                if first:
                    db_ref[:, gcols] = part_sum
                else:
                    db_ref[:, gcols] += part_sum

    @pl.when(s == 0)
    def _():
        for k in range(8):
            w_copy(k).start()
        if carried:
            dz_scr[1] = dz_in[...]
            fdc_ref[...] = fdc_in[...]
            db_ref[...] = db_in[...]
        else:
            step(True)
        for k in range(8):
            w_copy(k).wait()

    @pl.when(s >= (0 if carried else 1))
    def _():
        step(False)


def backward(e_parts, acts, w_t, rows, t_top, n_steps, widths, carry):
    total, hidden = acts.shape[1:]
    steps = total // rows
    n_e, n_blk = len(e_parts), hidden // 4
    out_rows = n_steps * rows
    half = steps // 2
    if n_e == 1:
        e_specs = [pl.BlockSpec((rows, hidden), lambda s: (t_top - s, 0))]
    else:
        e_specs = [
            pl.BlockSpec((rows, hidden), lambda s: (jnp.minimum(t_top - s, half - 1), 0)),
            pl.BlockSpec((rows, hidden), lambda s: (jnp.maximum(t_top - s - half, 0), 0)),
        ]
    in_specs = e_specs + [
        pl.BlockSpec((6, rows, hidden), lambda s: (0, t_top - s, 0)),
        pl.BlockSpec((1, rows, hidden), lambda s: (5, jnp.maximum(t_top - s - 1, 0), 0)),
    ]
    args = list(e_parts) + [acts, acts]
    if carry is not None:
        in_specs += [
            pl.BlockSpec((rows, 4 * hidden), lambda s: (0, 0)),
            pl.BlockSpec((rows, hidden), lambda s: (0, 0)),
            pl.BlockSpec((8, 4 * hidden), lambda s: (0, 0)),
        ]
        args += list(carry)
    in_specs.append(pl.BlockSpec(memory_space=pl.ANY))
    args.append(w_t)
    back = lambda s: (n_steps - 1 - s, 0)
    out_specs = [pl.BlockSpec((rows, 4 * hidden), back)]
    out_shape = [jax.ShapeDtypeStruct((out_rows, 4 * hidden), BF16)]
    for width in widths:
        out_specs.append(pl.BlockSpec((rows, width), back))
        out_shape.append(jax.ShapeDtypeStruct((out_rows, width), BF16))
    out_specs += [pl.BlockSpec((rows, hidden), lambda s: (0, 0)), pl.BlockSpec((8, 4 * hidden), lambda s: (0, 0))]
    out_shape += [jax.ShapeDtypeStruct((rows, hidden), F32), jax.ShapeDtypeStruct((8, 4 * hidden), F32)]
    outs = pl.pallas_call(
        functools.partial(backward_kernel, carry is not None, rows, t_top, n_e, widths, n_blk),
        grid=(n_steps,),
        in_specs=in_specs,
        out_specs=out_specs,
        out_shape=out_shape,
        scratch_shapes=[
            pltpu.VMEM((4 * hidden, hidden), BF16),
            pltpu.VMEM((2, rows, 4 * hidden), BF16),
            pltpu.SemaphoreType.DMA((8,)),
        ],
        compiler_params=pltpu.CompilerParams(dimension_semantics=("arbitrary",), vmem_limit_bytes=VMEM_BYTES),
        cost_estimate=pl.CostEstimate(flops=2 * out_rows * hidden * 4 * hidden, bytes_accessed=4 * hidden * hidden * 4, transcendentals=0),
    )(*args)
    return outs[0], outs[1 : 1 + len(widths)], outs[-2], outs[-1]


def weight_kernel(rows, n_piece, m_blk, aliased, core_ref, *refs):
    refs = list(refs)
    u_ref, h_ref = refs.pop(0), refs.pop(0)
    dz_refs = [refs.pop(0) for _ in range(n_piece)]
    if aliased:
        refs.pop(0)
    out_ref, send_ref, late = refs
    d, n_dev = pl.program_id(1), pl.num_programs(1)
    hidden = u_ref.shape[1]
    tall = dz_refs[0].shape[1]
    for k, ref in enumerate(dz_refs):
        skip = rows if k == 0 else 0
        late[pl.ds(k * tall + skip - rows, tall - skip), :] = ref[0, skip:, :]
    late[pl.ds(n_piece * tall - rows, rows), :] = jnp.zeros((rows, late.shape[1]), BF16)

    def share(m0):
        if m0 < hidden:
            total = dot(u_ref[0, pl.ds(m0, m_blk), 0:tall], dz_refs[0][0])
            for k in range(1, n_piece):
                total += dot(u_ref[0, pl.ds(m0, m_blk), k * tall : (k + 1) * tall], dz_refs[k][0])
        else:
            total = dot(h_ref[0, pl.ds(m0 - hidden, m_blk), :], late[...])
        return total.astype(BF16).astype(F32)

    @pl.when(d < n_dev - 1)
    def _():
        for m0 in range(0, 2 * hidden, m_blk):
            at = pl.ds(m0, m_blk)
            out_ref[0, at, :] = jnp.where(d == 0, 0.0, out_ref[0, at, :]) + share(m0)

    @pl.when(d == n_dev - 1)
    def _():
        for m0 in range(0, 2 * hidden, m_blk):
            at = pl.ds(m0, m_blk)
            low = (out_ref[0, at, :] + share(m0)).astype(BF16)
            out_ref[0, at, :] = low.astype(F32)
            send_ref[0, at, :] = low


def weight_grads(layer, col_blk, n_col, n_blk, core, u_all, h_all, dz_pieces, rows, out_shape, dw_acc):
    n_dev, hidden, total = u_all.shape
    tall = dz_pieces[0][0].shape[1]
    n_piece = len(dz_pieces)
    aliased = dw_acc is not None
    whole = pl.BlockSpec((1, hidden, total), lambda j, d, c: (d, 0, 0))
    in_specs = [whole, whole]
    for _, base in dz_pieces:
        in_specs.append(pl.BlockSpec((1, tall, n_blk), lambda j, d, c, base=base: (d, 0, base + 2 * j + c[0])))
    args = [core, u_all, h_all] + [a for a, _ in dz_pieces]
    aliases = {}
    if aliased:
        in_specs.append(pl.BlockSpec(memory_space=pl.ANY))
        aliases = {len(args): 0}
        args.append(dw_acc)
    return pl.pallas_call(
        functools.partial(weight_kernel, rows, n_piece, hidden // 4, aliased),
        grid_spec=pltpu.PrefetchScalarGridSpec(
            num_scalar_prefetch=1,
            grid=(n_col, n_dev),
            in_specs=in_specs,
            out_specs=[
                pl.BlockSpec((1, 2 * hidden, n_blk), lambda j, d, c: (layer, 0, col_blk + 2 * j + c[0])),
                pl.BlockSpec((1, 2 * hidden, n_blk), lambda j, d, c: (j, 0, 0)),
            ],
            scratch_shapes=[pltpu.VMEM((total, n_blk), BF16)],
        ),
        out_shape=[out_shape, jax.ShapeDtypeStruct((n_col, 2 * hidden, n_blk), BF16)],
        input_output_aliases=aliases,
        compiler_params=pltpu.CompilerParams(dimension_semantics=("arbitrary", "arbitrary"), vmem_limit_bytes=VMEM_BYTES),
        cost_estimate=pl.CostEstimate(flops=2 * n_dev * total * 2 * hidden * n_col * n_blk, bytes_accessed=n_col * 48 * 2**20, transcendentals=0),
    )(*args)


def widen_kernel(core_ref, recv_ref, dw_ref, out_ref):
    out_ref[...] = recv_ref[...].astype(F32)


def widen(layer, col_blk, core, recv, dw_acc):
    n_col, tall, n_blk = recv.shape
    m_blk = tall // 4
    return pl.pallas_call(
        widen_kernel,
        grid_spec=pltpu.PrefetchScalarGridSpec(
            num_scalar_prefetch=1,
            grid=(n_col, tall // m_blk),
            in_specs=[pl.BlockSpec((1, m_blk, n_blk), lambda j, m, c: (j, m, 0)), pl.BlockSpec(memory_space=pl.ANY)],
            out_specs=pl.BlockSpec((1, m_blk, n_blk), lambda j, m, c: (layer, m, col_blk + 2 * j + 1 - c[0])),
        ),
        out_shape=jax.ShapeDtypeStruct(dw_acc.shape, F32),
        input_output_aliases={2: 0},
        compiler_params=pltpu.CompilerParams(dimension_semantics=("arbitrary", "arbitrary")),
        cost_estimate=pl.CostEstimate(flops=n_col * tall * n_blk, bytes_accessed=6 * n_col * tall * n_blk, transcendentals=0),
    )(core, recv, dw_acc)


def transpose_kernel(a_ref, out_ref):
    out_ref[...] = a_ref[...].T


def transpose(a):
    tall, wide = a.shape
    blk = wide // 8
    return pl.pallas_call(
        transpose_kernel,
        grid=(8,),
        in_specs=[pl.BlockSpec((tall, blk), lambda k: (0, k))],
        out_specs=pl.BlockSpec((blk, tall), lambda k: (k, 0)),
        out_shape=jax.ShapeDtypeStruct((wide, tall), a.dtype),
        cost_estimate=pl.CostEstimate(flops=tall * wide, bytes_accessed=4 * tall * wide, transcendentals=0),
        name="transpose_x",
    )(a)


EARLY_WIDTHS = (1, 1, 1, 1)
LAST_WIDTHS = (1, 1, 1, 0.5, 0.5)


def solution(mesh):
    axes = ("replica", "data")
    n_data = mesh.shape["data"]
    swap = [(k, k ^ 1) for k in range(n_data)]

    def gather(a):
        return lax.all_gather(a, axes, axis=0, tiled=False)

    def body(x_loc, dy_loc, w_stack, b_stack):
        rows, steps, hidden = x_loc.shape
        total = rows * steps
        half = steps // 2
        n_blk = hidden // 4
        core = lax.rem(lax.axis_index("data"), 2).astype(jnp.int32)[None]
        dw_shape = jax.ShapeDtypeStruct(w_stack.shape, F32)
        early_widths = [int(hidden * w) for w in EARLY_WIDTHS]
        last_widths = [int(hidden * w) for w in LAST_WIDTHS]

        u_0 = jnp.swapaxes(x_loc, 0, 1).reshape(total, hidden)
        e_1 = jnp.swapaxes(dy_loc, 0, 1).reshape(total, hidden)
        x_all = gather(transpose(u_0))
        acts_0, u_1, h0_t, w_t0 = forward(0, u_0, w_stack, b_stack, rows, steps)
        h0_all = gather(h0_t)
        acts_1, _, h1_t, w_t1 = forward(1, u_1, w_stack, b_stack, rows, steps)
        h1_all = gather(h1_t)

        dz_late, _, fdc, db = backward([e_1], acts_1, w_t1, rows, steps - 1, half, (), None)
        late_all = gather(dz_late)
        dz_early, early, _, db_1 = backward([e_1], acts_1, w_t1, rows, half - 1, half, early_widths, (dz_late, fdc, db))
        early_all = [gather(a) for a in early]
        e_0 = [jnp.einsum("rg,hg->rh", dz, w_stack[1, :hidden], preferred_element_type=F32) for dz in (dz_early, dz_late)]
        dz_0, last, _, db_0 = backward(e_0, acts_0, w_t0, rows, steps - 1, steps, last_widths, None)
        last_all = [gather(a) for a in last]
        dx = jnp.einsum("rg,hg->rh", dz_0, w_stack[0, :hidden], preferred_element_type=F32)
        dx = jnp.swapaxes(dx.reshape(steps, rows, hidden), 0, 1)
        db_low = jnp.stack([jnp.sum(db_0, axis=0), jnp.sum(db_1, axis=0)]).astype(BF16).astype(F32)
        db_sum = lax.psum(db_low, axes)
        early_all[0], dx = lax.optimization_barrier((early_all[0], dx))

        jobs = []
        at = 0
        for k, width in enumerate(early_widths):
            jobs.append((1, at // n_blk, width, h0_all, h1_all, ((early_all[k], 0), (late_all, at // n_blk))))
            at += width
        at = 0
        for k, width in enumerate(last_widths):
            jobs.append((0, at // n_blk, width, x_all, h0_all, ((last_all[k], 0),)))
            at += width
        dw, waiting = None, None
        for layer, col, width, u_all, h_all, pieces in jobs:
            dw, own = weight_grads(layer, col, width // n_blk // 2, n_blk, core, u_all, h_all, pieces, rows, dw_shape, dw)
            other = lax.ppermute(own, "data", swap)
            if waiting is not None:
                dw = widen(waiting[0], waiting[1], core, waiting[2], dw)
            waiting = (layer, col, other)
        dw = widen(waiting[0], waiting[1], core, waiting[2], dw)
        return dw, db_sum, dx

    return jax.shard_map(body, mesh=mesh, in_specs=(P(axes), P(axes), P(), P()), out_specs=(P(), P(), P(axes)), check_vma=False)
```

time: 3650 us -> 1500 us (0.41)
  waiting for transfers between devices: 1920 us -> 364 us
  matrix products: 1130 us -> 66 us
  Pallas kernels: 0 us -> 1020 us
  other arithmetic: 388 us -> 2.75 us
  local copies, waits for them, and re-layouts: 163 us -> 20.5 us
    dot_general x72 -> x3, matrix products: 1130 us -> 66 us  [the longest x2 40.3 us: body(): jnp.einsum('rg,hg->rh', dz, w_stack[1, :hidden], preferred_element_type=F32)]
    pallas_call x0 -> x24, Pallas kernels: none -> 1020 us  [the longest x9 411 us: weight_grads(): pl.pallas_call(functools.partial(weight_kernel, rows, n_piece, hidden //...]
    psum x1, waiting for transfers between devices: 734 us -> 23.7 us  [body(): db_sum = lax.psum(db_low, axes)]
    unnamed x7 -> x14, waiting for transfers between devices: 455 us -> 4.97 us
    all_gather x2 -> x13, waiting for transfers between devices: 730 us -> 336 us  [gather(): return lax.all_gather(a, axes, axis=0, tiled=False)]
    concatenate x66 -> x0, other arithmetic: 178 us -> none  [the longest x2 90.8 us: layer_backward(): jnp.concatenate([dw_in, dw_rec], axis=0)]
    another operation x2 -> x0, other arithmetic: 128 us -> none  [the longest x1 127 us: local_grads(): jnp.stack(dw_list[::-1])]
    dynamic_update_slice x96 -> x0, other arithmetic: 79.3 us -> none  [the longest x64 52.4 us: layer_forward(): return lax.scan(time_step, init_state, in_proj)[1]]
  transfers between devices with their start and end apart: 5 -> 23, of which waited for: 5 -> 8; matrix products, arithmetic and copies ran while one was open for 13% -> 5% of each run, Pallas kernels for 0% -> 41%
where the time goes in v1:
time: 1500 us; the launch traced here: 1490 us
  Pallas kernels  1020 us (68%)
  waiting for transfers between devices  364 us (24%)
  matrix products  66 us (4%)
  local copies, waits for them, and re-layouts  20.5 us (1%)
    pallas_call x9, Pallas kernels, weight_grads(): pl.pallas_call(functools.partial(weight_kernel, rows, n_piece, hidden //...  411 us
    all_gather x13, waiting for transfers between devices, gather(): return lax.all_gather(a, axes, axis=0, tiled=False)  336 us
    pallas_call x2, Pallas kernels, forward(): pl.pallas_call(functools.partial(forward_kernel, layer, rows, steps, in_b...  296 us
    pallas_call x3, Pallas kernels, backward(): pl.pallas_call(functools.partial(backward_kernel, carry is not None, rows...  222 us
    pallas_call x9, Pallas kernels, widen(): pl.pallas_call(widen_kernel, grid_spec=pltpu.PrefetchScalarGridSpec(num_s...  85.5 us
    dot_general x2, matrix products, body(): jnp.einsum('rg,hg->rh', dz, w_stack[1, :hidden], preferred_element_type=F32)  40.3 us
  transfers between devices with their start and end apart: 23, of which 8 were waited for; matrix products, arithmetic and copies ran while one was open for 5% of the time, Pallas kernels for 41%

profile of v1, /device:TPU:0, one launch (start us, length us, event | category | flops | bytes accessed | tf_op | source)
XLA Modules:
  0.0 1490.8 jit_solution(863775532300902401)
XLA Ops:
  7.2 4.1 copy.24
  11.3 1.6 fusion.12
  12.9 6.6 copy.25
  19.5 146.9 %shard_map.67 = (f32[6,512,2048]{2,1,0:T(8,128)}, bf16[512,2048]{1,0:T(8,128)(2,1)}, bf16[2048,512]{1,0:T(8,128)(2,1)}, bf16[8192,2048]{1,0:T(8,128)(2,1)}) custom-call(bf16[512,2048]{1,0:T(8,128)(2,1)} %bitcast.59, bf16[2,4096,8192]{2,1,0:T(8,128)(2,1)} %w_hbm.3, f32[1,8192]{1,0:T(1,128)} %get-tuple-element.93.b_ref, bf16[2,4096,8192]{2,1,0:T(8,128)(2,1)} %w_hbm.3), custom_call_target="tpu_custom_call" | custom-call | flops 34359738368 | bytes 201326592 | tf_op jit(solution)/shard_map/pallas_call | solution.py:96
  166.5 148.6 %shard_map.68 = (f32[6,512,2048]{2,1,0:T(8,128)}, bf16[512,2048]{1,0:T(8,128)(2,1)}, bf16[2048,512]{1,0:T(8,128)(2,1)}, bf16[8192,2048]{1,0:T(8,128)(2,1)}) custom-call(bf16[512,2048]{1,0:T(8,128)(2,1)} %get-tuple-element.47.u_hbm, bf16[2,4096,8192]{2,1,0:T(8,128)(2,1)} %w_hbm.3, f32[1,8192]{1,0:T(1,128)} %get-tuple-element.92.b_ref, ...), custom_call_target="tpu_custom_call" | custom-call | flops 34359738368 | bytes 201326592 | tf_op jit(solution)/shard_map/pallas_call | solution.py:96
  315.1 55.1 %shard_map.69 = (bf16[256,8192]{1,0:T(8,128)(2,1)}, f32[32,2048]{1,0:T(8,128)}, f32[8,8192]{1,0:T(8,128)}) custom-call(f32[512,2048]{1,0:T(8,128)} %bitcast.57, f32[6,512,2048]{2,1,0:T(8,128)} %get-tuple-element.48.refs_1_.refs_2_, f32[6,512,2048]{2,1,0:T(8,128)} %get-tuple-element.48.refs_1_.refs_2_, bf16[8192,2048]{1,0:T(8,128)(2,1)} %get-tuple-element.49.refs_3_.refs_6_), custom_call_target="tpu_custom_call" | custom-call | flops 8589934592 | bytes 67108864 | tf_op jit(solution)/shard_map/pallas_call | solution.py:244
  370.2 62.0 %shard_map.70 = (bf16[256,8192]{1,0:T(8,128)(2,1)}, bf16[256,2048]{1,0:T(8,128)(2,1)}, bf16[256,2048]{1,0:T(8,128)(2,1)}, bf16[256,2048]{1,0:T(8,128)(2,1)}, bf1...) custom-call(f32[512,2048]{1,0:T(8,128)} %bitcast.58, ...), custom_call_target="tpu_custom_call" | custom-call | flops 8589934592 | bytes 67108864 | tf_op jit(solution)/shard_map/pallas_call | solution.py:244
  432.3 0.7 all-gather.29.cloned.1.call-update
  433.0 0.7 all-gather.37.cloned.1.call-update
  434.4 0.5 all-gather.45.cloned.1.call-update
  435.5 0.7 all-gather.47.cloned.1.call-update
  436.3 20.2 %fusion.2.refs_1_ = f32[256,2048]{1,0:T(8,128)} fusion(bf16[256,8192]{1,0:T(8,128)(2,1)} %get-tuple-element.50.refs_3_, bf16[2,4096,8192]{2,1,0:T(8,128)(2,1)} %w_hbm.3), kind=kOutput, calls=%fused_computation.2 | convolution fusion | flops 8589934592 | bytes 39845888 | tf_op jit(solution)/shard_map/rg,hg->rh/dot_general | solution.py:408
  456.4 20.1 %fusion.4.refs_0_ = f32[256,2048]{1,0:T(8,128)} fusion(bf16[256,8192]{1,0:T(8,128)(2,1)} %get-tuple-element.53, bf16[2,4096,8192]{2,1,0:T(8,128)(2,1)} %w_hbm.3), kind=kOutput, calls=%fused_computation.4 | convolution fusion | flops 8589934592 | bytes 39845888 | tf_op jit(solution)/shard_map/rg,hg->rh/dot_general | solution.py:408
  476.6 105.1 %shard_map.71 = (bf16[512,8192]{1,0:T(8,128)(2,1)}, bf16[512,2048]{1,0:T(8,128)(2,1)}, bf16[512,2048]{1,0:T(8,128)(2,1)}, bf16[512,2048]{1,0:T(8,128)(2,1)}, bf1...) custom-call(f32[256,2048]{1,0:T(8,128)} %fusion.4.refs_0_, ...), custom_call_target="tpu_custom_call" | custom-call | flops 17179869184 | bytes 67108864 | tf_op jit(solution)/shard_map/pallas_call | solution.py:244
  581.7 6.0 transpose_x.1
  588.4 0.7 all-gather.33.cloned.1.call-update
  589.2 25.7 %fusion.9 = f32[32,16,2048]{2,0,1:T(8,128)} fusion(bf16[16,32,8192]{2,1,0:T(8,128)(2,1)} %bitcast.72, bf16[2,4096,8192]{2,1,0:T(8,128)(2,1)} %w_hbm.3), kind=kOutput, calls=%fused_computation.9 | convolution fusion | flops 17179869184 | bytes 46137344 | tf_op jit(solution)/shard_map/rg,hg->rh/dot_general | solution.py:411
  614.9 41.1 %all-gather.37.cloned.1.call-done = bf16[16384,512]{1,0:T(8,128)(2,1)} async-done(((bf16[2048,512]{1,0:T(8,128)(2,1)}), bf16[16384,512]{1,0:T(8,128)(2,1)}) %all-gather.37.cloned.1.call-update) | async-done | bytes 16777232 | tf_op jit(solution)/shard_map/all_gather | solution.py:384
  656.0 156.8 %all-gather.41.cloned.1.call-done = bf16[2048,8192]{1,0:T(8,128)(2,1)} async-done(((bf16[256,8192]{1,0:T(8,128)(2,1)}), bf16[2048,8192]{1,0:T(8,128)(2,1)}) %all-gather.41.cloned.1.call-update) | async-done | bytes 33554448 | tf_op jit(solution)/shard_map/all_gather | solution.py:384
  812.8 50.4 %shard_map.72 = (f32[2,4096,8192]{2,1,0:T(8,128)}, bf16[2,4096,512]{2,1,0:T(8,128)(2,1)}) custom-call(s32[1]{0:T(128)} %bitcast.core_ref, bf16[8,2048,512]{2,1,0:T(8,128)(2,1)} %bitcast.35, bf16[8,2048,512]{2,1,0:T(8,128)(2,1)} %bitcast.53, bf16[8,256,2048]{2,1,0:T(8,128)(2,1)} %bitcast.71, bf16[8,256,8192]{2,1,0:T(8,128)(2,1)} %bitcast.49), custom_call_target="tpu_custom_call" | custom-call | flops 34359738368 | bytes 100663296 | tf_op jit(solution)/shard_map/pallas_call | solution.py:315
  863.4 50.3 %shard_map.73 = (f32[2,4096,8192]{2,1,0:T(8,128)}, bf16[2,4096,512]{2,1,0:T(8,128)(2,1)}) custom-call(s32[1]{0:T(128)} %bitcast.core_ref, bf16[8,2048,512]{2,1,0:T(8,128)(2,1)} %bitcast.36, bf16[8,2048,512]{2,1,0:T(8,128)(2,1)} %bitcast.54, bf16[8,256,2048]{2,1,0:T(8,128)(2,1)} %bitcast.66, ...), custom_call_target="tpu_custom_call", output_to_operand_aliasing={{0}: (5, {})} | custom-call | flops 34359738368 | bytes 100663296 | tf_op jit(solution)/shard_map/pallas_call | solution.py:315
  914.0 10.7 shard_map.74.refs_4_
  924.7 51.4 %shard_map.75 = (f32[2,4096,8192]{2,1,0:T(8,128)}, bf16[2,4096,512]{2,1,0:T(8,128)(2,1)}) custom-call(s32[1]{0:T(128)} %bitcast.core_ref, bf16[8,2048,512]{2,1,0:T(8,128)(2,1)} %bitcast.37, bf16[8,2048,512]{2,1,0:T(8,128)(2,1)} %bitcast.55, bf16[8,256,2048]{2,1,0:T(8,128)(2,1)} %bitcast.65, ...), custom_call_target="tpu_custom_call", output_to_operand_aliasing={{0}: (5, {})} | custom-call | flops 34359738368 | bytes 100663296 | tf_op jit(solution)/shard_map/pallas_call | solution.py:315
  976.7 10.3 shard_map.76.refs_4_
  987.0 51.2 %shard_map.77 = (f32[2,4096,8192]{2,1,0:T(8,128)}, bf16[2,4096,512]{2,1,0:T(8,128)(2,1)}) custom-call(s32[1]{0:T(128)} %bitcast.core_ref, bf16[8,2048,512]{2,1,0:T(8,128)(2,1)} %bitcast.38, bf16[8,2048,512]{2,1,0:T(8,128)(2,1)} %bitcast.56, bf16[8,256,2048]{2,1,0:T(8,128)(2,1)} %bitcast.64, ...), custom_call_target="tpu_custom_call", output_to_operand_aliasing={{0}: (5, {})} | custom-call | flops 34359738368 | bytes 100663296 | tf_op jit(solution)/shard_map/pallas_call | solution.py:315
  1038.2 10.3 shard_map.78.refs_3_
  1048.5 2.7 all-gather.35.cloned.1.call-done
  1051.3 86.6 %all-gather.27.cloned.1.call-done = bf16[16384,512]{1,0:T(8,128)(2,1)} async-done(((bf16[2048,512]{1,0:T(8,128)(2,1)}), bf16[16384,512]{1,0:T(8,128)(2,1)}) %all-gather.27.cloned.1.call-update) | async-done | bytes 16777232 | tf_op jit(solution)/shard_map/all_gather | solution.py:384
  1137.8 51.7 %shard_map.79 = (f32[2,4096,8192]{2,1,0:T(8,128)}, bf16[2,4096,512]{2,1,0:T(8,128)(2,1)}) custom-call(s32[1]{0:T(128)} %bitcast.core_ref, bf16[8,2048,512]{2,1,0:T(8,128)(2,1)} %bitcast.44, bf16[8,2048,512]{2,1,0:T(8,128)(2,1)} %bitcast.39, bf16[8,512,2048]{2,1,0:T(8,128)(2,1)} %bitcast.63, ...), custom_call_target="tpu_custom_call", output_to_operand_aliasing={{0}: (4, {})} | custom-call | flops 34359738368 | bytes 100663296 | tf_op jit(solution)/shard_map/pallas_call | solution.py:315
  1190.0 10.7 shard_map.80.refs_3_
  1200.8 23.0 %all-gather.49.cloned.1.call-done = bf16[4096,2048]{1,0:T(8,128)(2,1)} async-done(((bf16[512,2048]{1,0:T(8,128)(2,1)}), bf16[4096,2048]{1,0:T(8,128)(2,1)}) %all-gather.49.cloned.1.call-update) | async-done | bytes 16777232 | tf_op jit(solution)/shard_map/all_gather | solution.py:384
  1223.7 51.8 %shard_map.81 = (f32[2,4096,8192]{2,1,0:T(8,128)}, bf16[2,4096,512]{2,1,0:T(8,128)(2,1)}) custom-call(s32[1]{0:T(128)} %bitcast.core_ref, bf16[8,2048,512]{2,1,0:T(8,128)(2,1)} %bitcast.45, bf16[8,2048,512]{2,1,0:T(8,128)(2,1)} %bitcast.40, bf16[8,512,2048]{2,1,0:T(8,128)(2,1)} %bitcast.62, ...), custom_call_target="tpu_custom_call", output_to_operand_aliasing={{0}: (4, {})} | custom-call | flops 34359738368 | bytes 100663296 | tf_op jit(solution)/shard_map/pallas_call | solution.py:315
  1275.9 10.3 shard_map.82.refs_3_
  1286.3 23.5 %all-gather.33.cloned.1.call-done = bf16[4096,2048]{1,0:T(8,128)(2,1)} async-done(((bf16[512,2048]{1,0:T(8,128)(2,1)}), bf16[4096,2048]{1,0:T(8,128)(2,1)}) %all-gather.33.cloned.1.call-update) | async-done | bytes 16777232 | tf_op jit(solution)/shard_map/all_gather | solution.py:384
  1309.7 50.2 %shard_map.83 = (f32[2,4096,8192]{2,1,0:T(8,128)}, bf16[2,4096,512]{2,1,0:T(8,128)(2,1)}) custom-call(s32[1]{0:T(128)} %bitcast.core_ref, bf16[8,2048,512]{2,1,0:T(8,128)(2,1)} %bitcast.46, bf16[8,2048,512]{2,1,0:T(8,128)(2,1)} %bitcast.41, bf16[8,512,2048]{2,1,0:T(8,128)(2,1)} %bitcast.61, ...), custom_call_target="tpu_custom_call", output_to_operand_aliasing={{0}: (4, {})} | custom-call | flops 34359738368 | bytes 100663296 | tf_op jit(solution)/shard_map/pallas_call | solution.py:315
  1360.2 10.6 shard_map.84.refs_3_
  1370.8 27.3 %shard_map.85 = (f32[2,4096,8192]{2,1,0:T(8,128)}, bf16[1,4096,512]{2,1,0:T(8,128)(2,1)}) custom-call(s32[1]{0:T(128)} %bitcast.core_ref, bf16[8,2048,512]{2,1,0:T(8,128)(2,1)} %bitcast.47, bf16[8,2048,512]{2,1,0:T(8,128)(2,1)} %bitcast.42, bf16[8,512,1024]{2,1,0:T(8,128)(2,1)} %bitcast.67, ...), custom_call_target="tpu_custom_call", output_to_operand_aliasing={{0}: (4, {})} | custom-call | flops 17179869184 | bytes 50331648 | tf_op jit(solution)/shard_map/pallas_call | solution.py:315
  1398.2 10.5 shard_map.86.refs_3_
  1408.7 2.0 all-gather.31.cloned.1.call-done
  1410.7 26.5 %shard_map.87 = (f32[2,4096,8192]{2,1,0:T(8,128)}, bf16[1,4096,512]{2,1,0:T(8,128)(2,1)}) custom-call(s32[1]{0:T(128)} %bitcast.core_ref, bf16[8,2048,512]{2,1,0:T(8,128)(2,1)} %bitcast.48, bf16[8,2048,512]{2,1,0:T(8,128)(2,1)} %bitcast.43, bf16[8,512,1024]{2,1,0:T(8,128)(2,1)} %bitcast.68, ...), custom_call_target="tpu_custom_call", output_to_operand_aliasing={{0}: (4, {})} | custom-call | flops 17179869184 | bytes 50331648 | tf_op jit(solution)/shard_map/pallas_call | solution.py:315
  1437.5 1.0 reduce_sum.18
  1438.5 1.0 reduce_sum.19
  1439.6 0.7 maximum_convert_fusion
  1440.3 6.6 copy.26
  1446.9 6.0 shard_map.88.dw_ref
  1452.9 5.9 shard_map.89
  1458.8 23.7 %all-reduce.2.cloned.1.call-done = f32[2,8192]{1,0:T(2,128)} async-done(((f32[2,8192]{1,0:T(2,128)}), f32[2,8192]{1,0:T(2,128)}) %all-reduce.2.cloned.1.call-update) | async-done | bytes 65552 | tf_op jit(solution)/shard_map/psum | solution.py:414
  1482.6 1.5 copy.45
  (49 shorter events, 4.6 us)
Async XLA Ops:
  7.2 607.7 %all-gather.43.cloned.1.call-start = ((), (), s32[]{:S(2)}) async-start(), calls=%async_computation.9 | async-start | bytes 9437184 | tf_op jit(solution)/shard_map/all_gather | solution.py:384
  432.2 182.6 %all-gather.29.cloned.1.call-start = ((), (), s32[]{:S(2)}) async-start(), calls=%async_computation.2 | async-start | bytes 18874368 | tf_op jit(solution)/shard_map/all_gather | solution.py:384
  433.0 223.0 %all-gather.37.cloned.1.call-start = ((), (), s32[]{:S(2)}) async-start(), calls=%async_computation.6 | async-start | bytes 18874368 | tf_op jit(solution)/shard_map/all_gather | solution.py:384
  433.7 379.0 %all-gather.41.cloned.1.call-start = ((), (), s32[]{:S(2)}) async-start(), calls=%async_computation.8 | async-start | bytes 37748736 | tf_op jit(solution)/shard_map/all_gather | solution.py:384
  434.3 429.1 %all-gather.45.cloned.1.call-start = ((), (), s32[]{:S(2)}) async-start(), calls=%async_computation.10 | async-start | bytes 9437184 | tf_op jit(solution)/shard_map/all_gather | solution.py:384
  434.9 489.8 %all-gather.39.cloned.1.call-start = ((), (), s32[]{:S(2)}) async-start(), calls=%async_computation.7 | async-start | bytes 9437184 | tf_op jit(solution)/shard_map/all_gather | solution.py:384
  435.5 551.5 %all-gather.47.cloned.1.call-start = ((), (), s32[]{:S(2)}) async-start(), calls=%async_computation.11 | async-start | bytes 9437184 | tf_op jit(solution)/shard_map/all_gather | solution.py:384
  436.2 615.0 %all-gather.35.cloned.1.call-start = ((), (), s32[]{:S(2)}) async-start(), calls=%async_computation.5 | async-start | bytes 18874368 | tf_op jit(solution)/shard_map/all_gather | solution.py:384
  581.7 556.2 %all-gather.27.cloned.1.call-start = ((), (), s32[]{:S(2)}) async-start(), calls=%async_computation.1 | async-start | bytes 18874368 | tf_op jit(solution)/shard_map/all_gather | solution.py:384
  587.8 635.9 %all-gather.49.cloned.1.call-start = ((), (), s32[]{:S(2)}) async-start(), calls=%async_computation.12 | async-start | bytes 18874368 | tf_op jit(solution)/shard_map/all_gather | solution.py:384
  588.4 721.4 %all-gather.33.cloned.1.call-start = ((), (), s32[]{:S(2)}) async-start(), calls=%async_computation.4 | async-start | bytes 18874368 | tf_op jit(solution)/shard_map/all_gather | solution.py:384
  589.1 781.7 %all-gather.51.cloned.1.call-start = ((), (), s32[]{:S(2)}) async-start(), calls=%async_computation.13 | async-start | bytes 9437184 | tf_op jit(solution)/shard_map/all_gather | solution.py:384
  863.1 50.9 %collective-permute-start = (bf16[2,4096,512]{2,1,0:T(8,128)(2,1)}, bf16[2,4096,512]{2,1,0:T(8,128)(2,1)}, u32[]{:S(2)}, u32[]{:S(2)}) collective-permute-start(bf16[2,4096,512]{2,1,0:T(8,128)(2,1)} %get-tuple-element.64), channel_id=1, source_target_pairs={{0,1},{1,0},{2,3},{3,2},{4,5},{5,4},{6,7},{7,6}} | collective-permute-start | bytes 25165832 | tf_op jit(solution)/shard_map/ppermute | solution.py:429
  913.7 62.9 %collective-permute-start.2 = (bf16[2,4096,512]{2,1,0:T(8,128)(2,1)}, bf16[2,4096,512]{2,1,0:T(8,128)(2,1)}, u32[]{:S(2)}, u32[]{:S(2)}) collective-permute-start(bf16[2,4096,512]{2,1,0:T(8,128)(2,1)} %get-tuple-element.70), channel_id=1, source_target_pairs={{0,1},{1,0},{2,3},{3,2},{4,5},{5,4},{6,7},{7,6}} | collective-permute-start | bytes 25165832 | tf_op jit(solution)/shard_map/ppermute | solution.py:429
  976.2 62.0 %collective-permute-start.1 = (bf16[2,4096,512]{2,1,0:T(8,128)(2,1)}, bf16[2,4096,512]{2,1,0:T(8,128)(2,1)}, u32[]{:S(2)}, u32[]{:S(2)}) collective-permute-start(bf16[2,4096,512]{2,1,0:T(8,128)(2,1)} %get-tuple-element.68), channel_id=1, source_target_pairs={{0,1},{1,0},{2,3},{3,2},{4,5},{5,4},{6,7},{7,6}} | collective-permute-start | bytes 25165832 | tf_op jit(solution)/shard_map/ppermute | solution.py:429
  976.6 434.1 %all-gather.31.cloned.1.call-start = ((), (), s32[]{:S(2)}) async-start(), calls=%async_computation.3 | async-start | bytes 9437184 | tf_op jit(solution)/shard_map/all_gather | solution.py:384
  1038.2 151.9 %collective-permute-start.4 = (bf16[2,4096,512]{2,1,0:T(8,128)(2,1)}, bf16[2,4096,512]{2,1,0:T(8,128)(2,1)}, u32[]{:S(2)}, u32[]{:S(2)}) collective-permute-start(bf16[2,4096,512]{2,1,0:T(8,128)(2,1)} %get-tuple-element.75), channel_id=1, source_target_pairs={{0,1},{1,0},{2,3},{3,2},{4,5},{5,4},{6,7},{7,6}} | collective-permute-start | bytes 25165832 | tf_op jit(solution)/shard_map/ppermute | solution.py:429
  1189.5 86.4 %collective-permute-start.3 = (bf16[2,4096,512]{2,1,0:T(8,128)(2,1)}, bf16[2,4096,512]{2,1,0:T(8,128)(2,1)}, u32[]{:S(2)}, u32[]{:S(2)}) collective-permute-start(bf16[2,4096,512]{2,1,0:T(8,128)(2,1)} %get-tuple-element.73), channel_id=1, source_target_pairs={{0,1},{1,0},{2,3},{3,2},{4,5},{5,4},{6,7},{7,6}} | collective-permute-start | bytes 25165832 | tf_op jit(solution)/shard_map/ppermute | solution.py:429
  1190.0 292.6 %all-reduce.2.cloned.1.call-start = ((), (), s32[]{:S(2)}) async-start(), calls=%async_computation | async-start | bytes 131072 | tf_op jit(solution)/shard_map/psum | solution.py:414
  1275.6 84.6 %collective-permute-start.6 = (bf16[2,4096,512]{2,1,0:T(8,128)(2,1)}, bf16[2,4096,512]{2,1,0:T(8,128)(2,1)}, u32[]{:S(2)}, u32[]{:S(2)}) collective-permute-start(bf16[2,4096,512]{2,1,0:T(8,128)(2,1)} %get-tuple-element.80), channel_id=1, source_target_pairs={{0,1},{1,0},{2,3},{3,2},{4,5},{5,4},{6,7},{7,6}} | collective-permute-start | bytes 25165832 | tf_op jit(solution)/shard_map/ppermute | solution.py:429
  1359.9 38.2 %collective-permute-start.5 = (bf16[2,4096,512]{2,1,0:T(8,128)(2,1)}, bf16[2,4096,512]{2,1,0:T(8,128)(2,1)}, u32[]{:S(2)}, u32[]{:S(2)}) collective-permute-start(bf16[2,4096,512]{2,1,0:T(8,128)(2,1)} %get-tuple-element.78), channel_id=1, source_target_pairs={{0,1},{1,0},{2,3},{3,2},{4,5},{5,4},{6,7},{7,6}} | collective-permute-start | bytes 25165832 | tf_op jit(solution)/shard_map/ppermute | solution.py:429
  1398.1 48.8 %collective-permute-start.8 = (bf16[1,4096,512]{2,1,0:T(8,128)(2,1)}, bf16[1,4096,512]{2,1,0:T(8,128)(2,1)}, u32[]{:S(2)}, u32[]{:S(2)}) collective-permute-start(bf16[1,4096,512]{2,1,0:T(8,128)(2,1)} %get-tuple-element.84), channel_id=1, source_target_pairs={{0,1},{1,0},{2,3},{3,2},{4,5},{5,4},{6,7},{7,6}} | collective-permute-start | bytes 12582920 | tf_op jit(solution)/shard_map/ppermute | solution.py:429
  1437.2 15.7 %collective-permute-start.7 = (bf16[1,4096,512]{2,1,0:T(8,128)(2,1)}, bf16[1,4096,512]{2,1,0:T(8,128)(2,1)}, u32[]{:S(2)}, u32[]{:S(2)}) collective-permute-start(bf16[1,4096,512]{2,1,0:T(8,128)(2,1)} %get-tuple-element.83), channel_id=1, source_target_pairs={{0,1},{1,0},{2,3},{3,2},{4,5},{5,4},{6,7},{7,6}} | collective-permute-start | bytes 12582920 | tf_op jit(solution)/shard_map/ppermute | solution.py:429
Sparse Core Ops, SparseCore 0:
  432.4 51.4 all-gather.42
  485.7 84.1 all-gather.28
  571.7 84.1 all-gather.36
  657.6 155.0 all-gather.40
  814.4 48.6 all-gather.44
  864.8 48.6 all-gather.38
  915.4 48.6 all-gather.46
  965.9 85.2 all-gather.34
  1053.7 84.1 all-gather.26
  1139.5 84.1 all-gather.48
  1225.5 84.1 all-gather.32
  1311.4 48.6 all-gather.50
  1362.0 48.6 all-gather.30
  1440.4 42.0 all-reduce.1

commit v2 on v1

v2 whole, which is shorter than its diff:
```python
import functools

import jax
import jax.numpy as jnp
from jax import lax
from jax.experimental import pallas as pl
from jax.experimental.pallas import tpu as pltpu
from jax.sharding import PartitionSpec as P


VMEM_BYTES = 67043328
BF16, F32 = jnp.bfloat16, jnp.float32
FORWARD_REPEAT = (4, 2)
BACKWARD_REPEAT = (4, 3)
PIECES = {1: (2, 2), 0: (1.5, 1, 1, 0.5)}


def dot(a, b):
    return jnp.dot(a, b, preferred_element_type=F32)


def repeated_dot(a, b, repeat):
    rows = a.shape[0]
    many = dot(jnp.concatenate([a] * repeat, axis=0), b)
    out = many[:rows]
    for k in range(1, repeat):
        out = jnp.maximum(out, many[k * rows : (k + 1) * rows])
    return out


def forward_kernel(layer, rows, steps, in_blk, n_blk, repeat, u_hbm, win_ref, b_ref, w_hbm, acts_ref, h_hbm, ht_hbm, wt_hbm, wrec, zin, uh, c_scr, wt_buf, ht_buf, sem_w, sem_u, sem_o):
    hidden = uh.shape[1]
    n_in = 4 * hidden // in_blk
    cut = hidden // steps
    i = pl.program_id(0)
    part = hidden // 8

    def w_copy(k):
        return pltpu.make_async_copy(w_hbm.at[layer, pl.ds(hidden + k * part, part)], wrec.at[pl.ds(k * part, part)], sem_w.at[k])

    def wt_copy(t):
        return pltpu.make_async_copy(wt_buf, wt_hbm.at[t], sem_o.at[0])

    @pl.when(i == 0)
    def _():
        u_copy = pltpu.make_async_copy(u_hbm, uh, sem_u)
        u_copy.start()
        for k in range(8):
            w_copy(k).start()
        u_copy.wait()

    @pl.when(i < n_in)
    def _():
        zin[:, pl.ds(pl.multiple_of(i * in_blk, in_blk), in_blk)] = dot(uh[...], win_ref[0]) + b_ref[...]

    def step(t, first):
        now = pl.ds(pl.multiple_of(t * rows, rows), rows)
        wt_buf[...] = wrec[pl.ds(pl.multiple_of(t * cut, cut), cut), :].T
        h_prev = None if first else uh[pl.ds(pl.multiple_of((t - 1) * rows, rows), rows), :]
        for n0 in range(0, hidden, n_blk):
            cols = pl.ds(n0, n_blk)
            z = []
            for g in range(4):
                gcols = pl.ds(g * hidden + n0, n_blk)
                zg = zin[now, gcols]
                z.append(zg if first else zg + repeated_dot(h_prev, wrec[:, gcols], repeat))
            gate_i, gate_f, gate_g, gate_o = jax.nn.sigmoid(z[0]), jax.nn.sigmoid(z[1]), jnp.tanh(z[2]), jax.nn.sigmoid(z[3])
            c_new = gate_i * gate_g if first else gate_f * c_scr[:, cols] + gate_i * gate_g
            tanh_c = jnp.tanh(c_new)
            c_scr[:, cols] = c_new
            uh[now, cols] = (gate_o * tanh_c).astype(BF16)
            for k, a in enumerate((gate_i, gate_f, gate_g, gate_o, tanh_c, c_new)):
                acts_ref[k, :, cols] = a

    @pl.when(i == n_in)
    def _():
        for k in range(8):
            w_copy(k).wait()
        step(0, True)
        wt_copy(0).start()

    @pl.when(i > n_in)
    def _():
        t = i - n_in
        wt_copy(t - 1).wait()
        step(t, False)
        wt_copy(t).start()

    @pl.when(i == n_in + steps - 1)
    def _():
        h_copy = pltpu.make_async_copy(uh, h_hbm, sem_u)
        h_copy.start()
        for k in range(8):
            ht_buf[pl.ds(k * part, part), :] = uh[:, pl.ds(k * part, part)].T
        ht_copy = pltpu.make_async_copy(ht_buf, ht_hbm, sem_o.at[1])
        ht_copy.start()
        wt_copy(steps - 1).wait()
        h_copy.wait()
        ht_copy.wait()


def forward(layer, u, w_stack, b_stack, rows, steps):
    total, hidden = u.shape
    in_blk, n_blk = hidden // 4, hidden // 4
    n_in = 4 * hidden // in_blk
    t_of = lambda i: jnp.maximum(i - n_in, 0)
    k_of = lambda i: jnp.minimum(i, n_in - 1)
    return pl.pallas_call(
        functools.partial(forward_kernel, layer, rows, steps, in_blk, n_blk, FORWARD_REPEAT[layer]),
        grid=(n_in + steps,),
        in_specs=[
            pl.BlockSpec(memory_space=pl.ANY),
            pl.BlockSpec((1, hidden, in_blk), lambda i: (layer, 0, k_of(i))),
            pl.BlockSpec((1, in_blk), lambda i: (0, k_of(i))),
            pl.BlockSpec(memory_space=pl.ANY),
        ],
        out_specs=[
            pl.BlockSpec((6, rows, hidden), lambda i: (0, t_of(i), 0)),
            pl.BlockSpec(memory_space=pl.ANY),
            pl.BlockSpec(memory_space=pl.ANY),
            pl.BlockSpec(memory_space=pl.ANY),
        ],
        out_shape=[
            jax.ShapeDtypeStruct((6, total, hidden), F32),
            jax.ShapeDtypeStruct((total, hidden), BF16),
            jax.ShapeDtypeStruct((hidden, total), BF16),
            jax.ShapeDtypeStruct((steps, 4 * hidden, hidden // steps), BF16),
        ],
        scratch_shapes=[
            pltpu.VMEM((hidden, 4 * hidden), BF16),
            pltpu.VMEM((total, 4 * hidden), F32),
            pltpu.VMEM((total, hidden), BF16),
            pltpu.VMEM((rows, hidden), F32),
            pltpu.VMEM((4 * hidden, hidden // steps), BF16),
            pltpu.VMEM((hidden, total), BF16),
            pltpu.SemaphoreType.DMA((8,)),
            pltpu.SemaphoreType.DMA,
            pltpu.SemaphoreType.DMA((2,)),
        ],
        compiler_params=pltpu.CompilerParams(dimension_semantics=("arbitrary",), vmem_limit_bytes=VMEM_BYTES),
        cost_estimate=pl.CostEstimate(flops=4 * total * hidden * 4 * hidden, bytes_accessed=4 * hidden * hidden * 4 * 3, transcendentals=0),
    )(u, w_stack, b_stack[layer][None], w_stack)


def backward_kernel(rows, n_steps, widths, n_blk, repeat, e_ref, acts_ref, cprev_ref, wt_hbm, dz_ref, *refs):
    piece_refs = refs[: len(widths)]
    db_ref, fdc, wt, dz_scr, sem_w = refs[len(widths) :]
    starts = [sum(widths[:k]) for k in range(len(widths))]
    hidden = fdc.shape[1]
    n_slab, _, cut = wt.shape
    s = pl.program_id(0)
    t = n_steps - 1 - s

    def w_copy(k):
        return pltpu.make_async_copy(wt_hbm.at[k], wt.at[k], sem_w.at[k])

    def step(first):
        new, old = lax.rem(s, 2), lax.rem(s + 1, 2)
        later = None if first else dz_scr[old]
        for n0 in range(0, hidden, n_blk):
            cols = pl.ds(n0, n_blk)
            gate_i, gate_f, gate_g, gate_o, tanh_c = (acts_ref[k, :, cols] for k in range(5))
            c_prev = jnp.where(t > 0, cprev_ref[0, :, cols], 0.0)
            dh = e_ref[:, cols]
            if not first:
                w_cols = jnp.concatenate([wt[n0 // cut + k] for k in range(n_blk // cut)], axis=1)
                dh = dh + repeated_dot(later, w_cols, repeat)
            dc = dh * gate_o * (1.0 - tanh_c * tanh_c)
            if not first:
                dc = fdc[:, cols] + dc
            fdc[:, cols] = dc * gate_f
            dz = (
                dc * gate_g * gate_i * (1.0 - gate_i),
                dc * c_prev * gate_f * (1.0 - gate_f),
                dc * gate_i * (1.0 - gate_g * gate_g),
                dh * tanh_c * gate_o * (1.0 - gate_o),
            )
            for k in range(4):
                at = k * hidden + n0
                gcols = pl.ds(at, n_blk)
                low = dz[k].astype(BF16)
                dz_scr[new, :, gcols] = low
                dz_ref[:, gcols] = low
                for ref, start in zip(piece_refs, starts):
                    if start <= at < start + ref.shape[1]:
                        ref[:, pl.ds(at - start, n_blk)] = low
                part_sum = dz[k][0:8]
                for q in range(8, rows, 8):
                    part_sum = part_sum + dz[k][q : q + 8]
                if first:
                    db_ref[:, gcols] = part_sum
                else:
                    db_ref[:, gcols] += part_sum

    @pl.when(s == 0)
    def _():
        for k in range(n_slab):
            w_copy(k).start()
        step(True)
        for k in range(n_slab):
            w_copy(k).wait()

    @pl.when(s > 0)
    def _():
        step(False)


def backward(layer, e, acts, w_t, rows, widths):
    total, hidden = acts.shape[1:]
    steps = total // rows
    back = lambda s: (steps - 1 - s, 0)
    outs = pl.pallas_call(
        functools.partial(backward_kernel, rows, steps, widths, hidden // 8, BACKWARD_REPEAT[layer]),
        grid=(steps,),
        in_specs=[
            pl.BlockSpec((rows, hidden), back),
            pl.BlockSpec((6, rows, hidden), lambda s: (0, steps - 1 - s, 0)),
            pl.BlockSpec((1, rows, hidden), lambda s: (5, jnp.maximum(steps - 2 - s, 0), 0)),
            pl.BlockSpec(memory_space=pl.ANY),
        ],
        out_specs=[pl.BlockSpec((rows, w), back) for w in (4 * hidden, *widths)] + [pl.BlockSpec((8, 4 * hidden), lambda s: (0, 0))],
        out_shape=[jax.ShapeDtypeStruct((total, w), BF16) for w in (4 * hidden, *widths)] + [jax.ShapeDtypeStruct((8, 4 * hidden), F32)],
        scratch_shapes=[
            pltpu.VMEM((rows, hidden), F32),
            pltpu.VMEM(w_t.shape, BF16),
            pltpu.VMEM((2, rows, 4 * hidden), BF16),
            pltpu.SemaphoreType.DMA((steps,)),
        ],
        compiler_params=pltpu.CompilerParams(dimension_semantics=("arbitrary",), vmem_limit_bytes=VMEM_BYTES),
        cost_estimate=pl.CostEstimate(flops=2 * total * hidden * 4 * hidden, bytes_accessed=4 * hidden * hidden * 4, transcendentals=0),
    )(e, acts, acts, w_t)
    return outs[0], outs[1:-1], outs[-1]


def weight_kernel(rows, m_blk, aliased, core_ref, u_ref, h_ref, dz_ref, *refs):
    refs = list(refs)
    if aliased:
        refs.pop(0)
    out_ref, send_ref, later = refs
    d, n_dev = pl.program_id(1), pl.num_programs(1)
    hidden, total = u_ref.shape[1:]
    later[pl.ds(0, total - rows), :] = dz_ref[0, rows:, :]
    later[pl.ds(total - rows, rows), :] = jnp.zeros((rows, later.shape[1]), BF16)

    def share(m0):
        if m0 < hidden:
            total_sum = dot(u_ref[0, pl.ds(m0, m_blk), :], dz_ref[0])
        else:
            total_sum = dot(h_ref[0, pl.ds(m0 - hidden, m_blk), :], later[...])
        return total_sum.astype(BF16).astype(F32)

    @pl.when(d < n_dev - 1)
    def _():
        for m0 in range(0, 2 * hidden, m_blk):
            at = pl.ds(m0, m_blk)
            out_ref[0, at, :] = jnp.where(d == 0, 0.0, out_ref[0, at, :]) + share(m0)

    @pl.when(d == n_dev - 1)
    def _():
        for m0 in range(0, 2 * hidden, m_blk):
            at = pl.ds(m0, m_blk)
            low = (out_ref[0, at, :] + share(m0)).astype(BF16)
            out_ref[0, at, :] = low.astype(F32)
            send_ref[0, at, :] = low


def weight_grads(layer, col, n_blk, core, u_all, h_all, dz_all, rows, out_shape, dw):
    n_dev, hidden, total = u_all.shape
    n_col = dz_all.shape[2] // n_blk // 2
    whole = pl.BlockSpec((1, hidden, total), lambda j, d, c: (d, 0, 0))
    in_specs = [whole, whole, pl.BlockSpec((1, total, n_blk), lambda j, d, c: (d, 0, 2 * j + c[0]))]
    args = [core, u_all, h_all, dz_all]
    aliases = {}
    if dw is not None:
        in_specs.append(pl.BlockSpec(memory_space=pl.ANY))
        aliases = {len(args): 0}
        args.append(dw)
    return pl.pallas_call(
        functools.partial(weight_kernel, rows, hidden // 4, dw is not None),
        grid_spec=pltpu.PrefetchScalarGridSpec(
            num_scalar_prefetch=1,
            grid=(n_col, n_dev),
            in_specs=in_specs,
            out_specs=[
                pl.BlockSpec((1, 2 * hidden, n_blk), lambda j, d, c: (layer, 0, col // n_blk + 2 * j + c[0])),
                pl.BlockSpec((1, 2 * hidden, n_blk), lambda j, d, c: (j, 0, 0)),
            ],
            scratch_shapes=[pltpu.VMEM((total, n_blk), BF16)],
        ),
        out_shape=[out_shape, jax.ShapeDtypeStruct((n_col, 2 * hidden, n_blk), BF16)],
        input_output_aliases=aliases,
        compiler_params=pltpu.CompilerParams(dimension_semantics=("arbitrary", "arbitrary"), vmem_limit_bytes=VMEM_BYTES),
        cost_estimate=pl.CostEstimate(flops=2 * n_dev * total * 2 * hidden * n_col * n_blk, bytes_accessed=n_col * 48 * 2**20, transcendentals=0),
    )(*args)


def widen_kernel(core_ref, recv_ref, dw_ref, out_ref):
    out_ref[...] = recv_ref[...].astype(F32)


def widen(layer, col, core, recv, dw):
    n_col, tall, n_blk = recv.shape
    m_blk = tall // 4
    return pl.pallas_call(
        widen_kernel,
        grid_spec=pltpu.PrefetchScalarGridSpec(
            num_scalar_prefetch=1,
            grid=(n_col, tall // m_blk),
            in_specs=[pl.BlockSpec((1, m_blk, n_blk), lambda j, m, c: (j, m, 0)), pl.BlockSpec(memory_space=pl.ANY)],
            out_specs=pl.BlockSpec((1, m_blk, n_blk), lambda j, m, c: (layer, m, col // n_blk + 2 * j + 1 - c[0])),
        ),
        out_shape=jax.ShapeDtypeStruct(dw.shape, F32),
        input_output_aliases={2: 0},
        compiler_params=pltpu.CompilerParams(dimension_semantics=("arbitrary", "arbitrary")),
        cost_estimate=pl.CostEstimate(flops=n_col * tall * n_blk, bytes_accessed=6 * n_col * tall * n_blk, transcendentals=0),
    )(core, recv, dw)


def transpose_kernel(a_ref, out_ref):
    out_ref[...] = a_ref[...].T


def transpose(a):
    tall, wide = a.shape
    blk = wide // 8
    return pl.pallas_call(
        transpose_kernel,
        grid=(8,),
        in_specs=[pl.BlockSpec((tall, blk), lambda k: (0, k))],
        out_specs=pl.BlockSpec((blk, tall), lambda k: (k, 0)),
        out_shape=jax.ShapeDtypeStruct((wide, tall), a.dtype),
        cost_estimate=pl.CostEstimate(flops=tall * wide, bytes_accessed=4 * tall * wide, transcendentals=0),
        name="transpose_x",
    )(a)


def batch_major_kernel(a_ref, out_ref):
    out_ref[...] = jnp.swapaxes(a_ref[...], 0, 1)


def batch_major(a):
    steps, rows, hidden = a.shape
    blk = hidden // 8
    return pl.pallas_call(
        batch_major_kernel,
        grid=(8,),
        in_specs=[pl.BlockSpec((steps, rows, blk), lambda k: (0, 0, k))],
        out_specs=pl.BlockSpec((rows, steps, blk), lambda k: (0, 0, k)),
        out_shape=jax.ShapeDtypeStruct((rows, steps, hidden), a.dtype),
        cost_estimate=pl.CostEstimate(flops=steps * rows * hidden, bytes_accessed=8 * steps * rows * hidden, transcendentals=0),
        name="batch_major",
    )(a)


def solution(mesh):
    axes = ("replica", "data")
    n_data = mesh.shape["data"]
    swap = [(k, k ^ 1) for k in range(n_data)]

    def gather(a):
        return lax.all_gather(a, axes, axis=0, tiled=False)

    def body(x_loc, dy_loc, w_stack, b_stack):
        rows, steps, hidden = x_loc.shape
        total = rows * steps
        core = lax.rem(lax.axis_index("data"), 2).astype(jnp.int32)[None]
        dw_shape = jax.ShapeDtypeStruct(w_stack.shape, F32)
        widths = {layer: [int(hidden * w) for w in PIECES[layer]] for layer in PIECES}

        u_0 = jnp.swapaxes(x_loc, 0, 1).reshape(total, hidden)
        e_1 = jnp.swapaxes(dy_loc, 0, 1).reshape(total, hidden)
        x_all = gather(transpose(u_0))
        acts_0, u_1, h0_t, w_t0 = forward(0, u_0, w_stack, b_stack, rows, steps)
        h0_all = gather(h0_t)
        acts_1, _, h1_t, w_t1 = forward(1, u_1, w_stack, b_stack, rows, steps)
        h1_all = gather(h1_t)

        dz_1, pieces_1, db_1 = backward(1, e_1, acts_1, w_t1, rows, widths[1])
        all_1 = [gather(a) for a in pieces_1]
        e_0 = jnp.einsum("rg,hg->rh", dz_1, w_stack[1, :hidden], preferred_element_type=F32)
        dz_0, pieces_0, db_0 = backward(0, e_0, acts_0, w_t0, rows, widths[0])
        all_0 = [gather(a) for a in pieces_0]
        dx = jnp.einsum("rg,hg->rh", dz_0, w_stack[0, :hidden], preferred_element_type=F32)
        dx = batch_major(dx.reshape(steps, rows, hidden))
        db = [lax.psum(jnp.sum(a, axis=0).astype(BF16), axes).astype(F32) for a in (db_0, db_1)]
        all_1[0], dx, *db = lax.optimization_barrier((all_1[0], dx, *db))

        jobs = []
        for layer, gathered, u_all, h_all in ((1, all_1, h0_all, h1_all), (0, all_0, x_all, h0_all)):
            col = 0
            for width, dz_all in zip(widths[layer], gathered):
                jobs.append((layer, col, u_all, h_all, dz_all))
                col += width
        dw, waiting = None, []
        for layer, col, u_all, h_all, dz_all in jobs:
            dw, own = weight_grads(layer, col, hidden // 4, core, u_all, h_all, dz_all, rows, dw_shape, dw)
            waiting.append((layer, col, core, lax.ppermute(own, "data", swap)))
            if len(waiting) == 2:
                for other in waiting:
                    dw = widen(*other, dw)
                waiting = []
        return dw, jnp.stack(db), dx

    return jax.shard_map(body, mesh=mesh, in_specs=(P(axes), P(axes), P(), P()), out_specs=(P(), P(), P(axes)), check_vma=False)
```

time: 1500 us -> 1380 us (0.920)
  waiting for transfers between devices: 364 us -> 295 us
  Pallas kernels: 1020 us -> 956 us
  blocking collectives: 0 us -> 26.1 us
    all_gather x13 -> x9, waiting for transfers between devices: 336 us -> 286 us  [gather(): return lax.all_gather(a, axes, axis=0, tiled=False)]
    pallas_call x12 -> x9, Pallas kernels: 633 us -> 593 us  [the longest x6 401 us: weight_grads(): pl.pallas_call(functools.partial(weight_kernel, rows, hidden // 4, dw is...]
    psum x0 -> x1, blocking collectives: none -> 26.1 us  [body(): lax.psum(jnp.sum(a, axis=0).astype(BF16), axes).astype(F32)]
    psum x1 -> x0, waiting for transfers between devices: 23.7 us -> none  [body(): db_sum = lax.psum(db_low, axes)]
    pallas_call x2, Pallas kernels: 296 us -> 276 us  [forward(): pl.pallas_call(functools.partial(forward_kernel, layer, rows, steps, in_b...]
    dot_general x2 -> x1, matrix products: 40.3 us -> 28.1 us  [body(): jnp.einsum('rg,hg->rh', dz_1, w_stack[1, :hidden], preferred_element_type...]
    pallas_call x9 -> x6, Pallas kernels: 85.5 us -> 80.6 us  [widen(): pl.pallas_call(widen_kernel, grid_spec=pltpu.PrefetchScalarGridSpec(num_s...]
  transfers between devices with their start and end apart: 23 -> 15, of which waited for: 8 -> 8; matrix products, arithmetic and copies ran while one was open for 5% -> 4% of each run, Pallas kernels for 41% -> 42%
where the time goes in v2:
time: 1380 us; the launch traced here: 1370 us
  Pallas kernels  956 us (69%)
  waiting for transfers between devices  295 us (21%)
  matrix products  53.7 us (4%)
  blocking collectives  26.1 us (2%)
  between operations  14.3 us (1%)
    pallas_call x6, Pallas kernels, weight_grads(): pl.pallas_call(functools.partial(weight_kernel, rows, hidden // 4, dw is...  401 us
    all_gather x9, waiting for transfers between devices, gather(): return lax.all_gather(a, axes, axis=0, tiled=False)  286 us
    pallas_call x2, Pallas kernels, forward(): pl.pallas_call(functools.partial(forward_kernel, layer, rows, steps, in_b...  276 us
    pallas_call x2, Pallas kernels, backward(): pl.pallas_call(functools.partial(backward_kernel, rows, steps, widths, hi...  185 us
    pallas_call x6, Pallas kernels, widen(): pl.pallas_call(widen_kernel, grid_spec=pltpu.PrefetchScalarGridSpec(num_s...  80.6 us
    dot_general x1, matrix products, body(): jnp.einsum('rg,hg->rh', dz_1, w_stack[1, :hidden], preferred_element_type...  28.1 us
  transfers between devices with their start and end apart: 15, of which 8 were waited for; matrix products, arithmetic and copies ran while one was open for 4% of the time, Pallas kernels for 42%

profile of v2, /device:TPU:0, one launch (start us, length us, event | category | flops | bytes accessed | tf_op | source)
XLA Modules:
  0.0 1365.2 jit_solution(11609541138947520535)
XLA Ops:
  7.2 4.1 copy.18
  11.3 1.6 fusion.6
  12.9 6.6 copy.19
  19.5 127.7 %shard_map.67 = (f32[6,512,2048]{2,1,0:T(8,128)}, bf16[512,2048]{1,0:T(8,128)(2,1)}, bf16[2048,512]{1,0:T(8,128)(2,1)}, bf16[16,8192,128]{2,1,0:T(8,128)(2,1)}) custom-call(bf16[512,2048]{1,0:T(8,128)(2,1)} %bitcast.38, bf16[2,4096,8192]{2,1,0:T(8,128)(2,1)} %w_hbm.3, f32[1,8192]{1,0:T(1,128)} %get-tuple-element.72.b_ref, bf16[2,4096,8192]{2,1,0:T(8,128)(2,1)} %w_hbm.3), custom_call_target="tpu_custom_call" | custom-call | flops 34359738368 | bytes 201326592 | tf_op jit(solution)/shard_map/pallas_call | solution.py:108
  147.2 148.7 %shard_map.68 = (f32[6,512,2048]{2,1,0:T(8,128)}, bf16[512,2048]{1,0:T(8,128)(2,1)}, bf16[2048,512]{1,0:T(8,128)(2,1)}, bf16[16,8192,128]{2,1,0:T(8,128)(2,1)}) custom-call(bf16[512,2048]{1,0:T(8,128)(2,1)} %get-tuple-element.37.u_hbm, bf16[2,4096,8192]{2,1,0:T(8,128)(2,1)} %w_hbm.3, f32[1,8192]{1,0:T(1,128)} %get-tuple-element.71.b_ref, ...), custom_call_target="tpu_custom_call" | custom-call | flops 34359738368 | bytes 201326592 | tf_op jit(solution)/shard_map/pallas_call | solution.py:108
  295.9 98.7 %shard_map.69 = (bf16[512,8192]{1,0:T(8,128)(2,1)}, bf16[512,4096]{1,0:T(8,128)(2,1)}, bf16[512,4096]{1,0:T(8,128)(2,1)}, f32[8,8192]{1,0:T(8,128)}) custom-call(f32[512,2048]{1,0:T(8,128)} %bitcast.44, f32[6,512,2048]{2,1,0:T(8,128)} %get-tuple-element.38.acts_ref.cprev_ref, f32[6,512,2048]{2,1,0:T(8,128)} %get-tuple-element.38.acts_ref.cprev_ref, ...), custom_call_target="tpu_custom_call" | custom-call | flops 17179869184 | bytes 67108864 | tf_op jit(solution)/shard_map/pallas_call | solution.py:212
  394.7 0.7 all-gather.21.cloned.1.call-update
  395.5 0.7 all-gather.31.cloned.1.call-update
  396.2 0.5 all-gather.33.cloned.1.call-update
  396.8 6.1 transpose_x.1
  403.0 28.1 %fusion.2.e_ref = f32[512,2048]{1,0:T(8,128)} fusion(bf16[512,8192]{1,0:T(8,128)(2,1)} %get-tuple-element.40, bf16[2,4096,8192]{2,1,0:T(8,128)(2,1)} %w_hbm.3), kind=kOutput, calls=%fused_computation.2 | convolution fusion | flops 17179869184 | bytes 46137344 | tf_op jit(solution)/shard_map/rg,hg->rh/dot_general | solution.py:380
  431.0 86.5 %shard_map.70 = (bf16[512,8192]{1,0:T(8,128)(2,1)}, bf16[512,3072]{1,0:T(8,128)(2,1)}, bf16[512,2048]{1,0:T(8,128)(2,1)}, bf16[512,2048]{1,0:T(8,128)(2,1)}, bf1...) custom-call(f32[512,2048]{1,0:T(8,128)} %fusion.2.e_ref, f32[6,512,2048]{2,1,0:T(8,128)} %get-tuple-element.41.acts_ref.cprev_ref, ...), custom_call_target="tpu_custom_call" | custom-call | flops 17179869184 | bytes 67108864 | tf_op jit(solution)/shard_map/pallas_call | solution.py:212
  517.6 0.7 all-gather.27.cloned.1.call-update
  518.3 0.7 all-gather.25.cloned.1.call-update
  519.1 1.0 reduce_sum.18
  520.1 1.0 reduce_sum.19
  521.1 26.1 %all-reduce = (bf16[8192]{0:T(1024)(128)(2,1)S(1)}, bf16[8192]{0:T(1024)(128)(2,1)S(1)}) all-reduce(bf16[8192]{0:T(1024)(128)(2,1)S(1)} %reduce_sum.18, bf16[8192]{0:T(1024)(128)(2,1)S(1)} %reduce_sum.19), channel_id=1, replica_groups=mesh['replica'=2,'data'=4] {'replica','data'}, use_global_device_ids=true, to_apply=%region_1.0 | all-reduce | flops 16384 | bytes 65536 | tf_op jit(solution)/shard_map/psum | solution.py:385
  547.2 0.6 convert_element_type.13
  547.8 0.6 convert_element_type.15
  548.4 25.7 %fusion.a_ref = f32[16,32,2048]{2,1,0:T(8,128)} fusion(bf16[16,32,8192]{2,1,0:T(8,128)(2,1)} %bitcast.51, bf16[2,4096,8192]{2,1,0:T(8,128)(2,1)} %w_hbm.3), kind=kOutput, calls=%fused_computation | convolution fusion | flops 17179869184 | bytes 46137344 | tf_op jit(solution)/shard_map/rg,hg->rh/dot_general | solution.py:383
  574.1 6.8 batch_major.1
  580.9 59.2 %all-gather.21.cloned.1.call-done = bf16[16384,512]{1,0:T(8,128)(2,1)} async-done(((bf16[2048,512]{1,0:T(8,128)(2,1)}), bf16[16384,512]{1,0:T(8,128)(2,1)}) %all-gather.21.cloned.1.call-update) | async-done | bytes 16777232 | tf_op jit(solution)/shard_map/all_gather | solution.py:361
  640.1 86.0 %all-gather.31.cloned.1.call-done = bf16[16384,512]{1,0:T(8,128)(2,1)} async-done(((bf16[2048,512]{1,0:T(8,128)(2,1)}), bf16[16384,512]{1,0:T(8,128)(2,1)}) %all-gather.31.cloned.1.call-update) | async-done | bytes 16777232 | tf_op jit(solution)/shard_map/all_gather | solution.py:361
  726.2 99.1 %shard_map.71 = (f32[2,4096,8192]{2,1,0:T(8,128)}, bf16[4,4096,512]{2,1,0:T(8,128)(2,1)}) custom-call(s32[1]{0:T(128)} %bitcast.core_ref, bf16[8,2048,512]{2,1,0:T(8,128)(2,1)} %bitcast.26, bf16[8,2048,512]{2,1,0:T(8,128)(2,1)} %bitcast.42, bf16[8,512,4096]{2,1,0:T(8,128)(2,1)} %bitcast.50), custom_call_target="tpu_custom_call" | custom-call | flops 68719476736 | bytes 201326592 | tf_op jit(solution)/shard_map/pallas_call | solution.py:278
  825.2 0.4 collective-permute-start.1
  825.7 57.3 %all-gather.33.cloned.1.call-done = bf16[4096,4096]{1,0:T(8,128)(2,1)} async-done(((bf16[512,4096]{1,0:T(8,128)(2,1)}), bf16[4096,4096]{1,0:T(8,128)(2,1)}) %all-gather.33.cloned.1.call-update) | async-done | bytes 33554448 | tf_op jit(solution)/shard_map/all_gather | solution.py:361
  883.0 99.0 %shard_map.72 = (f32[2,4096,8192]{2,1,0:T(8,128)}, bf16[4,4096,512]{2,1,0:T(8,128)(2,1)}) custom-call(s32[1]{0:T(128)} %bitcast.core_ref, bf16[8,2048,512]{2,1,0:T(8,128)(2,1)} %bitcast.27, bf16[8,2048,512]{2,1,0:T(8,128)(2,1)} %bitcast.43, bf16[8,512,4096]{2,1,0:T(8,128)(2,1)} %bitcast.36, ...), custom_call_target="tpu_custom_call", output_to_operand_aliasing={{0}: (4, {})} | custom-call | flops 68719476736 | bytes 201326592 | tf_op jit(solution)/shard_map/pallas_call | solution.py:278
  982.0 0.4 collective-permute-start
  982.4 19.3 %shard_map.73.dw_ref = f32[2,4096,8192]{2,1,0:T(8,128)} custom-call(s32[1]{0:T(128)} %bitcast.core_ref, bf16[4,4096,512]{2,1,0:T(8,128)(2,1)} %collective-permute-done.1.recv_ref, f32[2,4096,8192]{2,1,0:T(8,128)} %get-tuple-element.57.dw_ref), custom_call_target="tpu_custom_call", output_to_operand_aliasing={{}: (2, {})} | custom-call | flops 8388608 | bytes 50331648 | tf_op jit(solution)/shard_map/pallas_call | solution.py:304
  1001.7 5.8 collective-permute-done.recv_ref
  1007.5 19.6 %shard_map.74.refs_0_ = f32[2,4096,8192]{2,1,0:T(8,128)} custom-call(s32[1]{0:T(128)} %bitcast.core_ref, bf16[4,4096,512]{2,1,0:T(8,128)(2,1)} %collective-permute-done.recv_ref, f32[2,4096,8192]{2,1,0:T(8,128)} %shard_map.73.dw_ref), custom_call_target="tpu_custom_call", output_to_operand_aliasing={{}: (2, {})} | custom-call | flops 8388608 | bytes 50331648 | tf_op jit(solution)/shard_map/pallas_call | solution.py:304
  1027.1 63.0 %all-gather.29.cloned.1.call-done = bf16[4096,3072]{1,0:T(8,128)(2,1)} async-done(((bf16[512,3072]{1,0:T(8,128)(2,1)}), bf16[4096,3072]{1,0:T(8,128)(2,1)}) %all-gather.29.cloned.1.call-update) | async-done | bytes 25165840 | tf_op jit(solution)/shard_map/all_gather | solution.py:361
  1090.2 74.8 %shard_map.75 = (f32[2,4096,8192]{2,1,0:T(8,128)}, bf16[3,4096,512]{2,1,0:T(8,128)(2,1)}) custom-call(s32[1]{0:T(128)} %bitcast.core_ref, bf16[8,2048,512]{2,1,0:T(8,128)(2,1)} %bitcast.32, bf16[8,2048,512]{2,1,0:T(8,128)(2,1)} %bitcast.28, bf16[8,512,3072]{2,1,0:T(8,128)(2,1)} %bitcast.37, ...), custom_call_target="tpu_custom_call", output_to_operand_aliasing={{0}: (4, {})} | custom-call | flops 51539607552 | bytes 150994944 | tf_op jit(solution)/shard_map/pallas_call | solution.py:278
  1165.0 0.4 collective-permute-start.3
  1165.5 11.8 all-gather.27.cloned.1.call-done
  1177.3 51.8 %shard_map.76 = (f32[2,4096,8192]{2,1,0:T(8,128)}, bf16[2,4096,512]{2,1,0:T(8,128)(2,1)}) custom-call(s32[1]{0:T(128)} %bitcast.core_ref, bf16[8,2048,512]{2,1,0:T(8,128)(2,1)} %bitcast.33, bf16[8,2048,512]{2,1,0:T(8,128)(2,1)} %bitcast.29, bf16[8,512,2048]{2,1,0:T(8,128)(2,1)} %bitcast.41, ...), custom_call_target="tpu_custom_call", output_to_operand_aliasing={{0}: (4, {})} | custom-call | flops 34359738368 | bytes 100663296 | tf_op jit(solution)/shard_map/pallas_call | solution.py:278
  1229.2 0.4 collective-permute-start.2
  1229.5 15.0 %shard_map.77.dw_ref = f32[2,4096,8192]{2,1,0:T(8,128)} custom-call(s32[1]{0:T(128)} %bitcast.core_ref, bf16[3,4096,512]{2,1,0:T(8,128)(2,1)} %collective-permute-done.3.recv_ref, f32[2,4096,8192]{2,1,0:T(8,128)} %get-tuple-element.61.dw_ref), custom_call_target="tpu_custom_call", output_to_operand_aliasing={{}: (2, {})} | custom-call | flops 6291456 | bytes 37748736 | tf_op jit(solution)/shard_map/pallas_call | solution.py:304
  1244.5 10.4 shard_map.78.refs_0_
  1255.0 8.4 all-gather.25.cloned.1.call-done
  1263.3 50.2 %shard_map.79 = (f32[2,4096,8192]{2,1,0:T(8,128)}, bf16[2,4096,512]{2,1,0:T(8,128)(2,1)}) custom-call(s32[1]{0:T(128)} %bitcast.core_ref, bf16[8,2048,512]{2,1,0:T(8,128)(2,1)} %bitcast.34, bf16[8,2048,512]{2,1,0:T(8,128)(2,1)} %bitcast.30, bf16[8,512,2048]{2,1,0:T(8,128)(2,1)} %bitcast.40, ...), custom_call_target="tpu_custom_call", output_to_operand_aliasing={{0}: (4, {})} | custom-call | flops 34359738368 | bytes 100663296 | tf_op jit(solution)/shard_map/pallas_call | solution.py:278
  1313.6 0.3 collective-permute-start.5
  1313.8 0.1 all-gather.23.cloned.1.call-done
  1313.9 26.4 %shard_map.80 = (f32[2,4096,8192]{2,1,0:T(8,128)}, bf16[1,4096,512]{2,1,0:T(8,128)(2,1)}) custom-call(s32[1]{0:T(128)} %bitcast.core_ref, bf16[8,2048,512]{2,1,0:T(8,128)(2,1)} %bitcast.35, bf16[8,2048,512]{2,1,0:T(8,128)(2,1)} %bitcast.31, bf16[8,512,1024]{2,1,0:T(8,128)(2,1)} %bitcast.45, ...), custom_call_target="tpu_custom_call", output_to_operand_aliasing={{0}: (4, {})} | custom-call | flops 17179869184 | bytes 50331648 | tf_op jit(solution)/shard_map/pallas_call | solution.py:278
  1340.3 0.2 collective-permute-start.4
  1340.6 1.5 pad_maximum_fusion
  1342.0 10.3 shard_map.81.dw_ref
  1352.3 5.9 shard_map.82
  (20 shorter events, 0.4 us)
Async XLA Ops:
  7.2 573.7 %all-gather.35.cloned.1.call-start = ((), (), s32[]{:S(2)}) async-start(), calls=%async_computation.8 | async-start | bytes 37748736 | tf_op jit(solution)/shard_map/all_gather | solution.py:361
  394.7 245.5 %all-gather.21.cloned.1.call-start = ((), (), s32[]{:S(2)}) async-start(), calls=%async_computation.1 | async-start | bytes 18874368 | tf_op jit(solution)/shard_map/all_gather | solution.py:361
  395.4 330.8 %all-gather.31.cloned.1.call-start = ((), (), s32[]{:S(2)}) async-start(), calls=%async_computation.6 | async-start | bytes 18874368 | tf_op jit(solution)/shard_map/all_gather | solution.py:361
  396.1 486.8 %all-gather.33.cloned.1.call-start = ((), (), s32[]{:S(2)}) async-start(), calls=%async_computation.7 | async-start | bytes 37748736 | tf_op jit(solution)/shard_map/all_gather | solution.py:361
  396.7 630.4 %all-gather.19.cloned.1.call-start = ((), (), s32[]{:S(2)}) async-start(), calls=%async_computation | async-start | bytes 18874368 | tf_op jit(solution)/shard_map/all_gather | solution.py:361
  402.9 687.3 %all-gather.29.cloned.1.call-start = ((), (), s32[]{:S(2)}) async-start(), calls=%async_computation.5 | async-start | bytes 28311552 | tf_op jit(solution)/shard_map/all_gather | solution.py:361
  517.5 659.8 %all-gather.27.cloned.1.call-start = ((), (), s32[]{:S(2)}) async-start(), calls=%async_computation.4 | async-start | bytes 18874368 | tf_op jit(solution)/shard_map/all_gather | solution.py:361
  518.3 745.1 %all-gather.25.cloned.1.call-start = ((), (), s32[]{:S(2)}) async-start(), calls=%async_computation.3 | async-start | bytes 18874368 | tf_op jit(solution)/shard_map/all_gather | solution.py:361
  519.0 794.9 %all-gather.23.cloned.1.call-start = ((), (), s32[]{:S(2)}) async-start(), calls=%async_computation.2 | async-start | bytes 9437184 | tf_op jit(solution)/shard_map/all_gather | solution.py:361
  825.2 157.2 %collective-permute-start.1 = (bf16[4,4096,512]{2,1,0:T(8,128)(2,1)}, bf16[4,4096,512]{2,1,0:T(8,128)(2,1)}, u32[]{:S(2)}, u32[]{:S(2)}) collective-permute-start(bf16[4,4096,512]{2,1,0:T(8,128)(2,1)} %get-tuple-element.56), channel_id=1, source_target_pairs={{0,1},{1,0},{2,3},{3,2},{4,5},{5,4},{6,7},{7,6}} | collective-permute-start | bytes 50331656 | tf_op jit(solution)/shard_map/ppermute | solution.py:397
  982.0 25.5 %collective-permute-start = (bf16[4,4096,512]{2,1,0:T(8,128)(2,1)}, bf16[4,4096,512]{2,1,0:T(8,128)(2,1)}, u32[]{:S(2)}, u32[]{:S(2)}) collective-permute-start(bf16[4,4096,512]{2,1,0:T(8,128)(2,1)} %get-tuple-element.55), channel_id=1, source_target_pairs={{0,1},{1,0},{2,3},{3,2},{4,5},{5,4},{6,7},{7,6}} | collective-permute-start | bytes 50331656 | tf_op jit(solution)/shard_map/ppermute | solution.py:397
  1165.0 64.5 %collective-permute-start.3 = (bf16[3,4096,512]{2,1,0:T(8,128)(2,1)}, bf16[3,4096,512]{2,1,0:T(8,128)(2,1)}, u32[]{:S(2)}, u32[]{:S(2)}) collective-permute-start(bf16[3,4096,512]{2,1,0:T(8,128)(2,1)} %get-tuple-element.60), channel_id=1, source_target_pairs={{0,1},{1,0},{2,3},{3,2},{4,5},{5,4},{6,7},{7,6}} | collective-permute-start | bytes 37748744 | tf_op jit(solution)/shard_map/ppermute | solution.py:397
  1229.2 15.4 %collective-permute-start.2 = (bf16[2,4096,512]{2,1,0:T(8,128)(2,1)}, bf16[2,4096,512]{2,1,0:T(8,128)(2,1)}, u32[]{:S(2)}, u32[]{:S(2)}) collective-permute-start(bf16[2,4096,512]{2,1,0:T(8,128)(2,1)} %get-tuple-element.59), channel_id=1, source_target_pairs={{0,1},{1,0},{2,3},{3,2},{4,5},{5,4},{6,7},{7,6}} | collective-permute-start | bytes 25165832 | tf_op jit(solution)/shard_map/ppermute | solution.py:397
  1313.6 28.4 %collective-permute-start.5 = (bf16[2,4096,512]{2,1,0:T(8,128)(2,1)}, bf16[2,4096,512]{2,1,0:T(8,128)(2,1)}, u32[]{:S(2)}, u32[]{:S(2)}) collective-permute-start(bf16[2,4096,512]{2,1,0:T(8,128)(2,1)} %get-tuple-element.64), channel_id=1, source_target_pairs={{0,1},{1,0},{2,3},{3,2},{4,5},{5,4},{6,7},{7,6}} | collective-permute-start | bytes 25165832 | tf_op jit(solution)/shard_map/ppermute | solution.py:397
  1340.3 12.0 collective-permute-start.4
Sparse Core Ops, SparseCore 0:
  394.8 159.2 all-gather.34
  555.9 84.1 all-gather.20
  642.0 84.1 all-gather.30
  727.8 155.0 all-gather.32
  884.6 84.1 all-gather.18
  970.5 119.6 all-gather.28
  1092.0 85.2 all-gather.26
  1179.1 84.1 all-gather.24
  1265.2 48.6 all-gather.22

commit v3 on v2

--- a/solution.py
+++ b/solution.py
@@ -10,8 +10,7 @@
 
 VMEM_BYTES = 67043328
 BF16, F32 = jnp.bfloat16, jnp.float32
-FORWARD_REPEAT = (4, 2)
-BACKWARD_REPEAT = (4, 3)
+REPEAT = 4
 PIECES = {1: (2, 2), 0: (1.5, 1, 1, 0.5)}
 
 
@@ -28,34 +27,41 @@
     return out
 
 
-def forward_kernel(layer, rows, steps, in_blk, n_blk, repeat, u_hbm, win_ref, b_ref, w_hbm, acts_ref, h_hbm, ht_hbm, wt_hbm, wrec, zin, uh, c_scr, wt_buf, ht_buf, sem_w, sem_u, sem_o):
+def forward_kernel(layer, rows, steps, in_blk, n_blk, repeat, u_hbm, win_ref, b_ref, w_hbm, acts_ref, h_hbm, ht_hbm, wt_hbm, wrec, zin, uh, c_scr, wt_buf, ht_buf, sem_w, sem_u, sem_o, sem_h):
     hidden = uh.shape[1]
     n_in = 4 * hidden // in_blk
     cut = hidden // steps
     i = pl.program_id(0)
     part = hidden // 8
 
+    w_part = hidden // n_in
+
     def w_copy(k):
-        return pltpu.make_async_copy(w_hbm.at[layer, pl.ds(hidden + k * part, part)], wrec.at[pl.ds(k * part, part)], sem_w.at[k])
+        at = pl.multiple_of(k * w_part, w_part)
+        return pltpu.make_async_copy(w_hbm.at[layer, pl.ds(hidden + at, w_part)], wrec.at[pl.ds(at, w_part)], sem_w.at[k])
 
     def wt_copy(t):
-        return pltpu.make_async_copy(wt_buf, wt_hbm.at[t], sem_o.at[0])
+        slot = lax.rem(t, 2)
+        return pltpu.make_async_copy(wt_buf.at[slot], wt_hbm.at[t], sem_o.at[slot])
+
+    def ht_copy(k):
+        slot = k % 2
+        return pltpu.make_async_copy(ht_buf.at[slot], ht_hbm.at[pl.ds(k * part, part)], sem_h.at[slot])
 
     @pl.when(i == 0)
     def _():
         u_copy = pltpu.make_async_copy(u_hbm, uh, sem_u)
         u_copy.start()
-        for k in range(8):
-            w_copy(k).start()
         u_copy.wait()
 
     @pl.when(i < n_in)
     def _():
+        w_copy(i).start()
         zin[:, pl.ds(pl.multiple_of(i * in_blk, in_blk), in_blk)] = dot(uh[...], win_ref[0]) + b_ref[...]
 
     def step(t, first):
         now = pl.ds(pl.multiple_of(t * rows, rows), rows)
-        wt_buf[...] = wrec[pl.ds(pl.multiple_of(t * cut, cut), cut), :].T
+        wt_buf[lax.rem(t, 2)] = wrec[pl.ds(pl.multiple_of(t * cut, cut), cut), :].T
         h_prev = None if first else uh[pl.ds(pl.multiple_of((t - 1) * rows, rows), rows), :]
         for n0 in range(0, hidden, n_blk):
             cols = pl.ds(n0, n_blk)
@@ -74,15 +80,19 @@
 
     @pl.when(i == n_in)
     def _():
-        for k in range(8):
+        for k in range(n_in):
             w_copy(k).wait()
-        step(0, True)
-        wt_copy(0).start()
+        step(i - n_in, True)
+        wt_copy(i - n_in).start()
 
     @pl.when(i > n_in)
     def _():
         t = i - n_in
-        wt_copy(t - 1).wait()
+
+        @pl.when(t > 1)
+        def _():
+            wt_copy(t - 2).wait()
+
         step(t, False)
         wt_copy(t).start()
 
@@ -91,12 +101,15 @@
         h_copy = pltpu.make_async_copy(uh, h_hbm, sem_u)
         h_copy.start()
         for k in range(8):
-            ht_buf[pl.ds(k * part, part), :] = uh[:, pl.ds(k * part, part)].T
-        ht_copy = pltpu.make_async_copy(ht_buf, ht_hbm, sem_o.at[1])
-        ht_copy.start()
+            if k >= 2:
+                ht_copy(k - 2).wait()
+            ht_buf[k % 2] = uh[:, pl.ds(k * part, part)].T
+            ht_copy(k).start()
+        wt_copy(steps - 2).wait()
         wt_copy(steps - 1).wait()
         h_copy.wait()
-        ht_copy.wait()
+        for k in range(6, 8):
+            ht_copy(k).wait()
 
 
 def forward(layer, u, w_stack, b_stack, rows, steps):
@@ -106,7 +119,7 @@
     t_of = lambda i: jnp.maximum(i - n_in, 0)
     k_of = lambda i: jnp.minimum(i, n_in - 1)
     return pl.pallas_call(
-        functools.partial(forward_kernel, layer, rows, steps, in_blk, n_blk, FORWARD_REPEAT[layer]),
+        functools.partial(forward_kernel, layer, rows, steps, in_blk, n_blk, REPEAT),
         grid=(n_in + steps,),
         in_specs=[
             pl.BlockSpec(memory_space=pl.ANY),
@@ -131,10 +144,11 @@
             pltpu.VMEM((total, 4 * hidden), F32),
             pltpu.VMEM((total, hidden), BF16),
             pltpu.VMEM((rows, hidden), F32),
-            pltpu.VMEM((4 * hidden, hidden // steps), BF16),
-            pltpu.VMEM((hidden, total), BF16),
-            pltpu.SemaphoreType.DMA((8,)),
+            pltpu.VMEM((2, 4 * hidden, hidden // steps), BF16),
+            pltpu.VMEM((2, hidden // 8, total), BF16),
+            pltpu.SemaphoreType.DMA((n_in,)),
             pltpu.SemaphoreType.DMA,
+            pltpu.SemaphoreType.DMA((2,)),
             pltpu.SemaphoreType.DMA((2,)),
         ],
         compiler_params=pltpu.CompilerParams(dimension_semantics=("arbitrary",), vmem_limit_bytes=VMEM_BYTES),
@@ -205,12 +219,12 @@
         step(False)
 
 
-def backward(layer, e, acts, w_t, rows, widths):
+def backward(e, acts, w_t, rows, widths):
     total, hidden = acts.shape[1:]
     steps = total // rows
     back = lambda s: (steps - 1 - s, 0)
     outs = pl.pallas_call(
-        functools.partial(backward_kernel, rows, steps, widths, hidden // 8, BACKWARD_REPEAT[layer]),
+        functools.partial(backward_kernel, rows, steps, widths, hidden // 8, REPEAT),
         grid=(steps,),
         in_specs=[
             pl.BlockSpec((rows, hidden), back),
@@ -375,10 +389,10 @@
         acts_1, _, h1_t, w_t1 = forward(1, u_1, w_stack, b_stack, rows, steps)
         h1_all = gather(h1_t)
 
-        dz_1, pieces_1, db_1 = backward(1, e_1, acts_1, w_t1, rows, widths[1])
+        dz_1, pieces_1, db_1 = backward(e_1, acts_1, w_t1, rows, widths[1])
         all_1 = [gather(a) for a in pieces_1]
         e_0 = jnp.einsum("rg,hg->rh", dz_1, w_stack[1, :hidden], preferred_element_type=F32)
-        dz_0, pieces_0, db_0 = backward(0, e_0, acts_0, w_t0, rows, widths[0])
+        dz_0, pieces_0, db_0 = backward(e_0, acts_0, w_t0, rows, widths[0])
         all_0 = [gather(a) for a in pieces_0]
         dx = jnp.einsum("rg,hg->rh", dz_0, w_stack[0, :hidden], preferred_element_type=F32)
         dx = batch_major(dx.reshape(steps, rows, hidden))

time: 1380 us -> 1300 us (0.942)
  Pallas kernels: 956 us -> 880 us
    pallas_call x2, Pallas kernels: 276 us -> 212 us  [forward(): pl.pallas_call(functools.partial(forward_kernel, layer, rows, steps, in_b...]
  transfers between devices with their start and end apart: 15 -> 15, of which waited for: 8 -> 8; matrix products, arithmetic and copies ran while one was open for 4% -> 5% of each run, Pallas kernels for 42% -> 45%
where the time goes in v3:
time: 1300 us; the launch traced here: 1290 us
  Pallas kernels  880 us (68%)
  waiting for transfers between devices  295 us (23%)
  matrix products  53.3 us (4%)
  blocking collectives  26.1 us (2%)
  between operations  14.3 us (1%)
    pallas_call x6, Pallas kernels, weight_grads(): pl.pallas_call(functools.partial(weight_kernel, rows, hidden // 4, dw is...  401 us
    all_gather x9, waiting for transfers between devices, gather(): return lax.all_gather(a, axes, axis=0, tiled=False)  286 us
    pallas_call x2, Pallas kernels, forward(): pl.pallas_call(functools.partial(forward_kernel, layer, rows, steps, in_b...  212 us
    pallas_call x2, Pallas kernels, backward(): pl.pallas_call(functools.partial(backward_kernel, rows, steps, widths, hi...  173 us
    pallas_call x6, Pallas kernels, widen(): pl.pallas_call(widen_kernel, grid_spec=pltpu.PrefetchScalarGridSpec(num_s...  80.6 us
    dot_general x1, matrix products, body(): jnp.einsum('rg,hg->rh', dz_1, w_stack[1, :hidden], preferred_element_type...  27.7 us
    psum x1, blocking collectives, body(): lax.psum(jnp.sum(a, axis=0).astype(BF16), axes).astype(F32)  26.1 us
  transfers between devices with their start and end apart: 15, of which 8 were waited for; matrix products, arithmetic and copies ran while one was open for 5% of the time, Pallas kernels for 45%

profile of v3, /device:TPU:0, one launch (start us, length us, event | category | flops | bytes accessed | tf_op | source)
XLA Modules:
  0.0 1288.6 jit_solution(10118752143795029622)
XLA Ops:
  7.2 4.1 copy.18
  11.3 1.6 fusion.6
  12.9 6.6 copy.19
  19.5 105.9 %shard_map.67 = (f32[6,512,2048]{2,1,0:T(8,128)}, bf16[512,2048]{1,0:T(8,128)(2,1)}, bf16[2048,512]{1,0:T(8,128)(2,1)}, bf16[16,8192,128]{2,1,0:T(8,128)(2,1)}) custom-call(bf16[512,2048]{1,0:T(8,128)(2,1)} %bitcast.38, bf16[2,4096,8192]{2,1,0:T(8,128)(2,1)} %w_hbm.3, f32[1,8192]{1,0:T(1,128)} %get-tuple-element.72.b_ref, bf16[2,4096,8192]{2,1,0:T(8,128)(2,1)} %w_hbm.3), custom_call_target="tpu_custom_call" | custom-call | flops 34359738368 | bytes 201326592 | tf_op jit(solution)/shard_map/pallas_call | solution.py:121
  125.4 106.1 %shard_map.68 = (f32[6,512,2048]{2,1,0:T(8,128)}, bf16[512,2048]{1,0:T(8,128)(2,1)}, bf16[2048,512]{1,0:T(8,128)(2,1)}, bf16[16,8192,128]{2,1,0:T(8,128)(2,1)}) custom-call(bf16[512,2048]{1,0:T(8,128)(2,1)} %get-tuple-element.37.u_hbm, bf16[2,4096,8192]{2,1,0:T(8,128)(2,1)} %w_hbm.3, f32[1,8192]{1,0:T(1,128)} %get-tuple-element.71.b_ref, ...), custom_call_target="tpu_custom_call" | custom-call | flops 34359738368 | bytes 201326592 | tf_op jit(solution)/shard_map/pallas_call | solution.py:121
  231.5 86.4 %shard_map.69 = (bf16[512,8192]{1,0:T(8,128)(2,1)}, bf16[512,4096]{1,0:T(8,128)(2,1)}, bf16[512,4096]{1,0:T(8,128)(2,1)}, f32[8,8192]{1,0:T(8,128)}) custom-call(f32[512,2048]{1,0:T(8,128)} %bitcast.44, f32[6,512,2048]{2,1,0:T(8,128)} %get-tuple-element.38.acts_ref.cprev_ref, f32[6,512,2048]{2,1,0:T(8,128)} %get-tuple-element.38.acts_ref.cprev_ref, ...), custom_call_target="tpu_custom_call" | custom-call | flops 17179869184 | bytes 67108864 | tf_op jit(solution)/shard_map/pallas_call | solution.py:226
  318.0 0.7 all-gather.21.cloned.1.call-update
  318.7 0.7 all-gather.31.cloned.1.call-update
  319.5 0.5 all-gather.33.cloned.1.call-update
  320.0 6.6 transpose_x.1
  326.7 27.7 %fusion.2.e_ref = f32[512,2048]{1,0:T(8,128)} fusion(bf16[512,8192]{1,0:T(8,128)(2,1)} %get-tuple-element.40, bf16[2,4096,8192]{2,1,0:T(8,128)(2,1)} %w_hbm.3), kind=kOutput, calls=%fused_computation.2 | convolution fusion | flops 17179869184 | bytes 46137344 | tf_op jit(solution)/shard_map/rg,hg->rh/dot_general | solution.py:394
  354.4 86.5 %shard_map.70 = (bf16[512,8192]{1,0:T(8,128)(2,1)}, bf16[512,3072]{1,0:T(8,128)(2,1)}, bf16[512,2048]{1,0:T(8,128)(2,1)}, bf16[512,2048]{1,0:T(8,128)(2,1)}, bf1...) custom-call(f32[512,2048]{1,0:T(8,128)} %fusion.2.e_ref, f32[6,512,2048]{2,1,0:T(8,128)} %get-tuple-element.41.acts_ref.cprev_ref, ...), custom_call_target="tpu_custom_call" | custom-call | flops 17179869184 | bytes 67108864 | tf_op jit(solution)/shard_map/pallas_call | solution.py:226
  440.9 0.7 all-gather.27.cloned.1.call-update
  441.6 0.7 all-gather.25.cloned.1.call-update
  442.4 1.0 reduce_sum.18
  443.4 1.0 reduce_sum.19
  444.4 26.1 %all-reduce = (bf16[8192]{0:T(1024)(128)(2,1)S(1)}, bf16[8192]{0:T(1024)(128)(2,1)S(1)}) all-reduce(bf16[8192]{0:T(1024)(128)(2,1)S(1)} %reduce_sum.18, bf16[8192]{0:T(1024)(128)(2,1)S(1)} %reduce_sum.19), channel_id=1, replica_groups=mesh['replica'=2,'data'=4] {'replica','data'}, use_global_device_ids=true, to_apply=%region_1.0 | all-reduce | flops 16384 | bytes 65536 | tf_op jit(solution)/shard_map/psum | solution.py:399
  470.5 0.6 convert_element_type.13
  471.2 0.6 convert_element_type.15
  471.8 25.7 %fusion.a_ref = f32[16,32,2048]{2,1,0:T(8,128)} fusion(bf16[16,32,8192]{2,1,0:T(8,128)(2,1)} %bitcast.51, bf16[2,4096,8192]{2,1,0:T(8,128)(2,1)} %w_hbm.3), kind=kOutput, calls=%fused_computation | convolution fusion | flops 17179869184 | bytes 46137344 | tf_op jit(solution)/shard_map/rg,hg->rh/dot_general | solution.py:397
  497.4 6.8 batch_major.1
  504.2 59.2 %all-gather.21.cloned.1.call-done = bf16[16384,512]{1,0:T(8,128)(2,1)} async-done(((bf16[2048,512]{1,0:T(8,128)(2,1)}), bf16[16384,512]{1,0:T(8,128)(2,1)}) %all-gather.21.cloned.1.call-update) | async-done | bytes 16777232 | tf_op jit(solution)/shard_map/all_gather | solution.py:375
  563.5 86.0 %all-gather.31.cloned.1.call-done = bf16[16384,512]{1,0:T(8,128)(2,1)} async-done(((bf16[2048,512]{1,0:T(8,128)(2,1)}), bf16[16384,512]{1,0:T(8,128)(2,1)}) %all-gather.31.cloned.1.call-update) | async-done | bytes 16777232 | tf_op jit(solution)/shard_map/all_gather | solution.py:375
  649.5 99.1 %shard_map.71 = (f32[2,4096,8192]{2,1,0:T(8,128)}, bf16[4,4096,512]{2,1,0:T(8,128)(2,1)}) custom-call(s32[1]{0:T(128)} %bitcast.core_ref, bf16[8,2048,512]{2,1,0:T(8,128)(2,1)} %bitcast.26, bf16[8,2048,512]{2,1,0:T(8,128)(2,1)} %bitcast.42, bf16[8,512,4096]{2,1,0:T(8,128)(2,1)} %bitcast.50), custom_call_target="tpu_custom_call" | custom-call | flops 68719476736 | bytes 201326592 | tf_op jit(solution)/shard_map/pallas_call | solution.py:292
  748.6 0.4 collective-permute-start.1
  749.0 57.3 %all-gather.33.cloned.1.call-done = bf16[4096,4096]{1,0:T(8,128)(2,1)} async-done(((bf16[512,4096]{1,0:T(8,128)(2,1)}), bf16[4096,4096]{1,0:T(8,128)(2,1)}) %all-gather.33.cloned.1.call-update) | async-done | bytes 33554448 | tf_op jit(solution)/shard_map/all_gather | solution.py:375
  806.3 99.0 %shard_map.72 = (f32[2,4096,8192]{2,1,0:T(8,128)}, bf16[4,4096,512]{2,1,0:T(8,128)(2,1)}) custom-call(s32[1]{0:T(128)} %bitcast.core_ref, bf16[8,2048,512]{2,1,0:T(8,128)(2,1)} %bitcast.27, bf16[8,2048,512]{2,1,0:T(8,128)(2,1)} %bitcast.43, bf16[8,512,4096]{2,1,0:T(8,128)(2,1)} %bitcast.36, ...), custom_call_target="tpu_custom_call", output_to_operand_aliasing={{0}: (4, {})} | custom-call | flops 68719476736 | bytes 201326592 | tf_op jit(solution)/shard_map/pallas_call | solution.py:292
  905.4 0.4 collective-permute-start
  905.7 19.3 %shard_map.73.dw_ref = f32[2,4096,8192]{2,1,0:T(8,128)} custom-call(s32[1]{0:T(128)} %bitcast.core_ref, bf16[4,4096,512]{2,1,0:T(8,128)(2,1)} %collective-permute-done.1.recv_ref, f32[2,4096,8192]{2,1,0:T(8,128)} %get-tuple-element.57.dw_ref), custom_call_target="tpu_custom_call", output_to_operand_aliasing={{}: (2, {})} | custom-call | flops 8388608 | bytes 50331648 | tf_op jit(solution)/shard_map/pallas_call | solution.py:318
  925.0 5.8 collective-permute-done.recv_ref
  930.9 19.6 %shard_map.74.refs_0_ = f32[2,4096,8192]{2,1,0:T(8,128)} custom-call(s32[1]{0:T(128)} %bitcast.core_ref, bf16[4,4096,512]{2,1,0:T(8,128)(2,1)} %collective-permute-done.recv_ref, f32[2,4096,8192]{2,1,0:T(8,128)} %shard_map.73.dw_ref), custom_call_target="tpu_custom_call", output_to_operand_aliasing={{}: (2, {})} | custom-call | flops 8388608 | bytes 50331648 | tf_op jit(solution)/shard_map/pallas_call | solution.py:318
  950.5 63.1 %all-gather.29.cloned.1.call-done = bf16[4096,3072]{1,0:T(8,128)(2,1)} async-done(((bf16[512,3072]{1,0:T(8,128)(2,1)}), bf16[4096,3072]{1,0:T(8,128)(2,1)}) %all-gather.29.cloned.1.call-update) | async-done | bytes 25165840 | tf_op jit(solution)/shard_map/all_gather | solution.py:375
  1013.5 74.8 %shard_map.75 = (f32[2,4096,8192]{2,1,0:T(8,128)}, bf16[3,4096,512]{2,1,0:T(8,128)(2,1)}) custom-call(s32[1]{0:T(128)} %bitcast.core_ref, bf16[8,2048,512]{2,1,0:T(8,128)(2,1)} %bitcast.32, bf16[8,2048,512]{2,1,0:T(8,128)(2,1)} %bitcast.28, bf16[8,512,3072]{2,1,0:T(8,128)(2,1)} %bitcast.37, ...), custom_call_target="tpu_custom_call", output_to_operand_aliasing={{0}: (4, {})} | custom-call | flops 51539607552 | bytes 150994944 | tf_op jit(solution)/shard_map/pallas_call | solution.py:292
  1088.3 0.5 collective-permute-start.3
  1088.8 11.8 all-gather.27.cloned.1.call-done
  1100.7 51.8 %shard_map.76 = (f32[2,4096,8192]{2,1,0:T(8,128)}, bf16[2,4096,512]{2,1,0:T(8,128)(2,1)}) custom-call(s32[1]{0:T(128)} %bitcast.core_ref, bf16[8,2048,512]{2,1,0:T(8,128)(2,1)} %bitcast.33, bf16[8,2048,512]{2,1,0:T(8,128)(2,1)} %bitcast.29, bf16[8,512,2048]{2,1,0:T(8,128)(2,1)} %bitcast.41, ...), custom_call_target="tpu_custom_call", output_to_operand_aliasing={{0}: (4, {})} | custom-call | flops 34359738368 | bytes 100663296 | tf_op jit(solution)/shard_map/pallas_call | solution.py:292
  1152.5 0.4 collective-permute-start.2
  1152.9 15.0 %shard_map.77.dw_ref = f32[2,4096,8192]{2,1,0:T(8,128)} custom-call(s32[1]{0:T(128)} %bitcast.core_ref, bf16[3,4096,512]{2,1,0:T(8,128)(2,1)} %collective-permute-done.3.recv_ref, f32[2,4096,8192]{2,1,0:T(8,128)} %get-tuple-element.61.dw_ref), custom_call_target="tpu_custom_call", output_to_operand_aliasing={{}: (2, {})} | custom-call | flops 6291456 | bytes 37748736 | tf_op jit(solution)/shard_map/pallas_call | solution.py:318
  1167.9 10.4 shard_map.78.refs_0_
  1178.3 8.4 all-gather.25.cloned.1.call-done
  1186.7 50.2 %shard_map.79 = (f32[2,4096,8192]{2,1,0:T(8,128)}, bf16[2,4096,512]{2,1,0:T(8,128)(2,1)}) custom-call(s32[1]{0:T(128)} %bitcast.core_ref, bf16[8,2048,512]{2,1,0:T(8,128)(2,1)} %bitcast.34, bf16[8,2048,512]{2,1,0:T(8,128)(2,1)} %bitcast.30, bf16[8,512,2048]{2,1,0:T(8,128)(2,1)} %bitcast.40, ...), custom_call_target="tpu_custom_call", output_to_operand_aliasing={{0}: (4, {})} | custom-call | flops 34359738368 | bytes 100663296 | tf_op jit(solution)/shard_map/pallas_call | solution.py:292
  1236.9 0.3 collective-permute-start.5
  1237.2 0.1 all-gather.23.cloned.1.call-done
  1237.2 26.4 %shard_map.80 = (f32[2,4096,8192]{2,1,0:T(8,128)}, bf16[1,4096,512]{2,1,0:T(8,128)(2,1)}) custom-call(s32[1]{0:T(128)} %bitcast.core_ref, bf16[8,2048,512]{2,1,0:T(8,128)(2,1)} %bitcast.35, bf16[8,2048,512]{2,1,0:T(8,128)(2,1)} %bitcast.31, bf16[8,512,1024]{2,1,0:T(8,128)(2,1)} %bitcast.45, ...), custom_call_target="tpu_custom_call", output_to_operand_aliasing={{0}: (4, {})} | custom-call | flops 17179869184 | bytes 50331648 | tf_op jit(solution)/shard_map/pallas_call | solution.py:292
  1263.6 0.2 collective-permute-start.4
  1263.9 1.5 pad_maximum_fusion
  1265.4 10.3 shard_map.81.dw_ref
  1275.7 5.9 shard_map.82
  (20 shorter events, 0.4 us)
Async XLA Ops:
  7.2 497.1 %all-gather.35.cloned.1.call-start = ((), (), s32[]{:S(2)}) async-start(), calls=%async_computation.8 | async-start | bytes 37748736 | tf_op jit(solution)/shard_map/all_gather | solution.py:375
  317.9 245.5 %all-gather.21.cloned.1.call-start = ((), (), s32[]{:S(2)}) async-start(), calls=%async_computation.1 | async-start | bytes 18874368 | tf_op jit(solution)/shard_map/all_gather | solution.py:375
  318.7 330.8 %all-gather.31.cloned.1.call-start = ((), (), s32[]{:S(2)}) async-start(), calls=%async_computation.6 | async-start | bytes 18874368 | tf_op jit(solution)/shard_map/all_gather | solution.py:375
  319.4 486.9 %all-gather.33.cloned.1.call-start = ((), (), s32[]{:S(2)}) async-start(), calls=%async_computation.7 | async-start | bytes 37748736 | tf_op jit(solution)/shard_map/all_gather | solution.py:375
  320.0 630.5 %all-gather.19.cloned.1.call-start = ((), (), s32[]{:S(2)}) async-start(), calls=%async_computation | async-start | bytes 18874368 | tf_op jit(solution)/shard_map/all_gather | solution.py:375
  326.6 686.9 %all-gather.29.cloned.1.call-start = ((), (), s32[]{:S(2)}) async-start(), calls=%async_computation.5 | async-start | bytes 28311552 | tf_op jit(solution)/shard_map/all_gather | solution.py:375
  440.8 659.8 %all-gather.27.cloned.1.call-start = ((), (), s32[]{:S(2)}) async-start(), calls=%async_computation.4 | async-start | bytes 18874368 | tf_op jit(solution)/shard_map/all_gather | solution.py:375
  441.6 745.1 %all-gather.25.cloned.1.call-start = ((), (), s32[]{:S(2)}) async-start(), calls=%async_computation.3 | async-start | bytes 18874368 | tf_op jit(solution)/shard_map/all_gather | solution.py:375
  442.3 794.9 %all-gather.23.cloned.1.call-start = ((), (), s32[]{:S(2)}) async-start(), calls=%async_computation.2 | async-start | bytes 9437184 | tf_op jit(solution)/shard_map/all_gather | solution.py:375
  748.6 157.2 %collective-permute-start.1 = (bf16[4,4096,512]{2,1,0:T(8,128)(2,1)}, bf16[4,4096,512]{2,1,0:T(8,128)(2,1)}, u32[]{:S(2)}, u32[]{:S(2)}) collective-permute-start(bf16[4,4096,512]{2,1,0:T(8,128)(2,1)} %get-tuple-element.56), channel_id=1, source_target_pairs={{0,1},{1,0},{2,3},{3,2},{4,5},{5,4},{6,7},{7,6}} | collective-permute-start | bytes 50331656 | tf_op jit(solution)/shard_map/ppermute | solution.py:411
  905.4 25.5 %collective-permute-start = (bf16[4,4096,512]{2,1,0:T(8,128)(2,1)}, bf16[4,4096,512]{2,1,0:T(8,128)(2,1)}, u32[]{:S(2)}, u32[]{:S(2)}) collective-permute-start(bf16[4,4096,512]{2,1,0:T(8,128)(2,1)} %get-tuple-element.55), channel_id=1, source_target_pairs={{0,1},{1,0},{2,3},{3,2},{4,5},{5,4},{6,7},{7,6}} | collective-permute-start | bytes 50331656 | tf_op jit(solution)/shard_map/ppermute | solution.py:411
  1088.3 64.5 %collective-permute-start.3 = (bf16[3,4096,512]{2,1,0:T(8,128)(2,1)}, bf16[3,4096,512]{2,1,0:T(8,128)(2,1)}, u32[]{:S(2)}, u32[]{:S(2)}) collective-permute-start(bf16[3,4096,512]{2,1,0:T(8,128)(2,1)} %get-tuple-element.60), channel_id=1, source_target_pairs={{0,1},{1,0},{2,3},{3,2},{4,5},{5,4},{6,7},{7,6}} | collective-permute-start | bytes 37748744 | tf_op jit(solution)/shard_map/ppermute | solution.py:411
  1152.5 15.4 %collective-permute-start.2 = (bf16[2,4096,512]{2,1,0:T(8,128)(2,1)}, bf16[2,4096,512]{2,1,0:T(8,128)(2,1)}, u32[]{:S(2)}, u32[]{:S(2)}) collective-permute-start(bf16[2,4096,512]{2,1,0:T(8,128)(2,1)} %get-tuple-element.59), channel_id=1, source_target_pairs={{0,1},{1,0},{2,3},{3,2},{4,5},{5,4},{6,7},{7,6}} | collective-permute-start | bytes 25165832 | tf_op jit(solution)/shard_map/ppermute | solution.py:411
  1236.9 28.4 %collective-permute-start.5 = (bf16[2,4096,512]{2,1,0:T(8,128)(2,1)}, bf16[2,4096,512]{2,1,0:T(8,128)(2,1)}, u32[]{:S(2)}, u32[]{:S(2)}) collective-permute-start(bf16[2,4096,512]{2,1,0:T(8,128)(2,1)} %get-tuple-element.64), channel_id=1, source_target_pairs={{0,1},{1,0},{2,3},{3,2},{4,5},{5,4},{6,7},{7,6}} | collective-permute-start | bytes 25165832 | tf_op jit(solution)/shard_map/ppermute | solution.py:411
  1263.6 12.0 collective-permute-start.4
Sparse Core Ops, SparseCore 0:
  318.1 159.3 all-gather.34
  479.3 84.1 all-gather.20
  565.3 84.1 all-gather.30
  651.2 155.0 all-gather.32
  808.0 84.1 all-gather.18
  893.8 119.6 all-gather.28
  1015.3 85.2 all-gather.26
  1102.5 84.1 all-gather.24
  1188.5 48.6 all-gather.22
